TPU v7x, 128 devices: a whole 4x4x4 slice. The times are simulated.
128 devices in a mesh: dp: 2 (over core), seq: 64 (over z, x, y).
Axes of the slice: x: 4, y: 4, z: 4, core: 2. Of those that a mesh axis runs over, the one named last changes fastest.
Arguments:
- queries: bfloat16 [2, 16384, 2048], P('dp', 'seq'), may hold values from -6 to 6
- keys: bfloat16 [2, 16384, 2048], P('dp', 'seq'), may hold values from -6 to 6
- values: bfloat16 [2, 16384, 2048], P('dp', 'seq'), may hold values from -6 to 6
- out_grad: bfloat16 [2, 16384, 4096], P('dp', 'seq'), may hold values from -6 to 6
- out_weight: bfloat16 [2048, 4096], replicated, may hold values from -0.125 to 0.125
Outputs:
- attended: bfloat16 [2, 16384, 2048], P('dp', 'seq')
- query_grad: bfloat16 [2, 16384, 2048], P('dp', 'seq')
- key_grad: bfloat16 [2, 16384, 2048], P('dp', 'seq')
- value_grad: bfloat16 [2, 16384, 2048], P('dp', 'seq')
- weight_grad: float32 [2048, 4096], P(('dp', 'seq'))
All inputs are finite; a program needn't handle non-finite values.
Results may differ from a plain program's by a relative error of at most 0.0051.
Values sent between devices are 32-bit elements; how exact they have to be, the bound alone decides.
A program may use at most 192 MiB of HBM per device.

v0:
```python
import jax
import jax.numpy as jnp
from jax import lax
from jax.sharding import Mesh
from jax.sharding import PartitionSpec as P

P_SIZE = 128
H = 16
HD = 2048
SEQ = ("seq_0", "seq_1", "seq_2")
DP_SEQ = ("dp", "seq_0", "seq_1", "seq_2")


EPS = 1e-06
HIGH = lax.Precision.HIGHEST


def filled_with(x, identity):
    return jnp.zeros_like(x) + jnp.asarray(identity, x.dtype)


def carried_in(x, axes, combine, identity, reverse):
    before = start = filled_with(x, identity)
    total = x
    for axis in reversed(axes):
        length, mine = (lax.axis_size(axis), lax.axis_index(axis))
        pieces = lax.all_gather(total, axis)
        inside, total = (start, start)
        for k in reversed(range(length)) if reverse else range(length):
            passed = k > mine if reverse else k < mine
            total = combine(total, pieces[k])
            inside = jnp.where(passed, total, inside)
        before = combine(inside, before)
    return before


def adding(earlier, later):
    return earlier + later


def body(queries, keys, values, out_grad, out_weight):
    query = queries[0]
    count = query.shape[0]
    heads_shape = (count, H, P_SIZE)
    q_heads = query.reshape(heads_shape)
    k_heads = keys[0].reshape(heads_shape)
    v_heads = values[0].reshape(heads_shape)
    cotangent = out_grad[0]
    state = jnp.einsum("shp,she->hpe", k_heads, v_heads, preferred_element_type=jnp.float32)
    blank = jnp.zeros_like(state)
    prefix = carried_in(state, SEQ, adding, blank, False)
    lower = (
        lax.broadcasted_iota(jnp.int32, (count, count), 0)
        >= lax.broadcasted_iota(jnp.int32, (count, count), 1)
    )[None]
    scores = jnp.einsum("thp,shp->hts", q_heads, k_heads, preferred_element_type=jnp.float32)
    probs = jnp.where(lower, scores, 0.0).astype(jnp.bfloat16)
    intra = jnp.einsum("hts,shp->thp", probs, v_heads, preferred_element_type=jnp.float32)
    q_float = q_heads.astype(jnp.float32)
    inter = jnp.einsum("thp,hpe->the", q_float, prefix, precision=HIGH)
    outputs = intra + inter
    inverse = lax.rsqrt(jnp.mean(outputs * outputs, axis=-1, keepdims=True) + EPS)
    normed = outputs * inverse
    attended = normed.astype(jnp.bfloat16)
    grad = jnp.einsum(
        "td,rd->tr", cotangent, out_weight, preferred_element_type=jnp.float32
    ).reshape(heads_shape)
    d_out = (inverse * (grad - normed * jnp.mean(grad * normed, axis=-1, keepdims=True))).astype(
        jnp.bfloat16
    )
    d_scores = jnp.einsum("the,she->hts", d_out, v_heads, preferred_element_type=jnp.float32)
    d_probs = jnp.where(lower, d_scores, 0.0).astype(jnp.bfloat16)
    d_prefix = jnp.einsum("thp,the->hpe", q_heads, d_out, preferred_element_type=jnp.float32)
    suffix = carried_in(d_prefix, SEQ, adding, blank, True)
    d_query = jnp.einsum("hts,shp->thp", d_probs, k_heads, preferred_element_type=jnp.float32)
    d_query = d_query + jnp.einsum(
        "the,hpe->thp", d_out.astype(jnp.float32), prefix, precision=HIGH
    )
    d_key = jnp.einsum("hts,thp->shp", d_probs, q_heads, preferred_element_type=jnp.float32)
    d_key = d_key + jnp.einsum("she,hpe->shp", v_heads.astype(jnp.float32), suffix, precision=HIGH)
    d_value = jnp.einsum("hts,the->she", probs, d_out, preferred_element_type=jnp.float32)
    d_value = d_value + jnp.einsum(
        "shp,hpe->she", k_heads.astype(jnp.float32), suffix, precision=HIGH
    )
    flat_shape = (1, count, HD)
    attended_rows = attended.reshape(count, HD)
    half_rows = lax.psum_scatter(
        jnp.einsum("tr,td->rd", attended_rows, cotangent, preferred_element_type=jnp.float32),
        "dp",
        scatter_dimension=0,
        tiled=True,
    )
    weight_grad = lax.psum_scatter(half_rows, SEQ, scatter_dimension=0, tiled=True)
    return (
        attended.reshape(flat_shape),
        d_query.astype(jnp.bfloat16).reshape(flat_shape),
        d_key.astype(jnp.bfloat16).reshape(flat_shape),
        d_value.astype(jnp.bfloat16).reshape(flat_shape),
        weight_grad,
    )


def solution(mesh):
    split = Mesh(mesh.devices.reshape(mesh.shape["dp"], 4, 4, 4), ("dp", "seq_0", "seq_1", "seq_2"))
    in_specs = (P("dp", SEQ, None), P("dp", SEQ, None), P("dp", SEQ, None), P("dp", SEQ, None), P())
    out_specs = (
        P("dp", SEQ, None),
        P("dp", SEQ, None),
        P("dp", SEQ, None),
        P("dp", SEQ, None),
        P(DP_SEQ, None),
    )
    return jax.shard_map(body, mesh=split, in_specs=in_specs, out_specs=out_specs, check_vma=False)
```

profile of v0, /device:TPU:0, one launch (start us, length us, event | category | flops | bytes accessed | tf_op | source)
XLA Modules:
  0.0 792.9 jit_solution(6475845321016397381)
XLA Ops:
  7.2 1.6 copy.57
  8.8 1.6 copy.34
  13.5 50.8 %all-gather.17.cloned.1.call-done = f32[64,128,128]{2,1,0:T(8,128)} async-done(((f32[16,128,128]{2,1,0:T(8,128)}), f32[64,128,128]{2,1,0:T(8,128)}) %all-gather.17.cloned.1.call-update) | async-done | bytes 4194320 | tf_op jit(solution)/shard_map/all_gather | solution.py:27
  64.3 3.4 fusion.13
  67.8 48.6 %all-gather.9.cloned.1.call-done = f32[4,16,128,128]{3,2,1,0:T(8,128)} async-done(((f32[1,16,128,128]{3,2,1,0:T(8,128)}), f32[4,16,128,128]{3,2,1,0:T(8,128)}) %all-gather.9.cloned.1.call-update) | async-done | bytes 4194320 | tf_op jit(solution)/shard_map/all_gather | solution.py:27
  116.4 3.4 slice_add_fusion.12
  123.8 2.1 fusion.18
  126.0 42.8 %all-gather.11.cloned.1.call-done = f32[4,16,128,128]{3,2,1,0:T(8,128)} async-done(((f32[1,16,128,128]{3,2,1,0:T(8,128)}), f32[4,16,128,128]{3,2,1,0:T(8,128)}) %all-gather.11.cloned.1.call-update) | async-done | bytes 4194320 | tf_op jit(solution)/shard_map/all_gather | solution.py:27
  168.8 6.2 fusion.12
  176.4 8.2 %multiply_reduce_fusion = (f32[256,16]{0,1:T(8,128)S(1)}, f32[256,16,128]{0,2,1:T(8,128)S(1)}) fusion(f32[256,16,128]{0,2,1:T(8,128)S(1)} %get-tuple-element.18, f32[256,16]{0,1:T(8,128)S(1)} %add_rsqrt_fusion, bf16[16,128,4096]{2,1,0:T(8,128)(2,1)} %bitcast.102, bf16[1,256,4096]{2,1,0:T(8,128)(2,1)S(1)} %copy-done), kind=kOutput, calls=%fused_computation.13 | convolution fusion | flops 4296536064 | bytes 23101440 | tf_op jit(solution)/shard_map/td,rd->tr/dot_general | solution.py:65
  184.7 1.6 multiply_convert_fusion
  187.7 2.5 copy.44
  190.3 48.5 %all-gather.19.cloned.1.call-done = f32[64,128,128]{2,1,0:T(8,128)} async-done(((f32[16,128,128]{2,1,0:T(8,128)}), f32[64,128,128]{2,1,0:T(8,128)}) %all-gather.19.cloned.1.call-update) | async-done | bytes 4194320 | tf_op jit(solution)/shard_map/all_gather | solution.py:27
  238.8 3.4 fusion.9
  242.5 15.3 %fusion.4 = f32[2048,4096]{1,0:T(8,128)} fusion(bf16[256,2048]{0,1:T(8,128)(2,1)} %bitcast.91, bf16[1,256,4096]{2,1,0:T(8,128)(2,1)S(1)} %copy-done), kind=kOutput, calls=%fused_computation.8 | convolution fusion | flops 4294967296 | bytes 36700160 | tf_op jit(solution)/shard_map/tr,td->rd/dot_general | solution.py:88
  257.8 33.1 %all-gather.13.cloned.1.call-done = f32[4,16,128,128]{3,2,1,0:T(8,128)} async-done(((f32[1,16,128,128]{3,2,1,0:T(8,128)}), f32[4,16,128,128]{3,2,1,0:T(8,128)}) %all-gather.13.cloned.1.call-update) | async-done | bytes 4194320 | tf_op jit(solution)/shard_map/all_gather | solution.py:27
  290.9 3.5 slice_add_fusion.3
  294.5 44.3 %reduce-scatter.3.cloned.1.call-done = f32[1024,4096]{1,0:T(8,128)} async-done(((f32[2048,4096]{1,0:T(8,128)}), f32[1024,4096]{1,0:T(8,128)}) %reduce-scatter.3.cloned.1.call-update) | async-done | bytes 16777232 | tf_op jit(solution)/shard_map/reduce_scatter | solution.py:87
  347.2 3.4 fusion.30
  350.6 39.7 %all-gather.15.cloned.1.call-done = f32[4,16,128,128]{3,2,1,0:T(8,128)} async-done(((f32[1,16,128,128]{3,2,1,0:T(8,128)}), f32[4,16,128,128]{3,2,1,0:T(8,128)}) %all-gather.15.cloned.1.call-update) | async-done | bytes 4194320 | tf_op jit(solution)/shard_map/all_gather | solution.py:27
  390.3 6.2 fusion.8
  396.5 2.1 add_convert_fusion
  398.7 2.3 copy.51
  405.1 381.0 %reduce-scatter.5.cloned.1.call-done = f32[16,4096]{1,0:T(8,128)} async-done(((f32[1024,4096]{1,0:T(8,128)}), f32[16,4096]{1,0:T(8,128)}) %reduce-scatter.5.cloned.1.call-update) | async-done | bytes 262160 | tf_op jit(solution)/shard_map/reduce_scatter | solution.py:93
  (75 shorter events, 22.7 us)
Async XLA Ops:
  7.2 169.3 %copy-start = (bf16[1,256,4096]{2,1,0:T(8,128)(2,1)S(1)}, bf16[1,256,4096]{2,1,0:T(8,128)(2,1)}, u32[]{:S(2)}) copy-start(bf16[1,256,4096]{2,1,0:T(8,128)(2,1)} %param.8) | copy-start | bytes 6291460
  7.2 57.1 %all-gather.17.cloned.1.call-start = ((), (), s32[]{:S(2)}) async-start(), calls=%async_computation.8 | async-start | bytes 5242880 | tf_op jit(solution)/shard_map/all_gather | solution.py:27
  8.8 1.6 copy-start.11
  10.4 1.6 copy-start.9
  12.0 110.4 %copy-start.2 = (bf16[32,8,16,128]{3,2,1,0:T(8,128)(2,1)}, bf16[32,8,16,128]{3,2,1,0:T(8,128)(2,1)S(1)}, u32[]{:S(2)}) copy-start(bf16[32,8,16,128]{3,2,1,0:T(8,128)(2,1)S(1)} %copy.58) | copy-start | bytes 3145732
  13.4 103.0 %all-gather.9.cloned.1.call-start = ((), (), s32[]{:S(2)}) async-start(), calls=%async_computation.2 | async-start | bytes 5242880 | tf_op jit(solution)/shard_map/all_gather | solution.py:27
  67.8 101.0 %all-gather.11.cloned.1.call-start = ((), (), s32[]{:S(2)}) async-start(), calls=%async_computation.3 | async-start | bytes 5242880 | tf_op jit(solution)/shard_map/all_gather | solution.py:27
  119.9 118.9 %all-gather.19.cloned.1.call-start = ((), (), s32[]{:S(2)}) async-start(), calls=%async_computation.9 | async-start | bytes 5242880 | tf_op jit(solution)/shard_map/all_gather | solution.py:27
  119.9 1.6 copy-start.12
  122.5 1.3 copy-start.19
  126.0 49.0 %copy-start.5 = (bf16[32,8,16,128]{3,2,1,0:T(8,128)(2,1)S(1)}, bf16[32,8,16,128]{3,2,1,0:T(8,128)(2,1)}, u32[]{:S(2)}) copy-start(bf16[32,8,16,128]{3,2,1,0:T(8,128)(2,1)} %copy-done.4) | copy-start | bytes 3145732
  168.8 6.2 copy-start.18
  175.0 1.4 copy-start.14
  184.7 1.6 copy-start.6
  190.3 100.7 %all-gather.13.cloned.1.call-start = ((), (), s32[]{:S(2)}) async-start(), calls=%async_computation.4 | async-start | bytes 5242880 | tf_op jit(solution)/shard_map/all_gather | solution.py:27
  242.3 96.5 %reduce-scatter.3.cloned.1.call-start = ((), (), s32[]{:S(2)}) async-start(), calls=%async_computation.6 | async-start | bytes 50331648 | tf_op jit(solution)/shard_map/reduce_scatter | solution.py:87
  257.8 132.5 %all-gather.15.cloned.1.call-start = ((), (), s32[]{:S(2)}) async-start(), calls=%async_computation.5 | async-start | bytes 5242880 | tf_op jit(solution)/shard_map/all_gather | solution.py:27
  294.4 491.6 %reduce-scatter.5.cloned.1.call-start = ((), (), s32[]{:S(2)}) async-start(), calls=%async_computation.7 | async-start | bytes 17039360 | tf_op jit(solution)/shard_map/reduce_scatter | solution.py:93
  338.8 2.6 copy-start.3
  342.7 2.0 copy-start.15
  350.6 45.9 %copy-start.13 = (bf16[32,8,16,128]{3,2,1,0:T(8,128)(2,1)S(1)}, bf16[32,8,16,128]{3,2,1,0:T(8,128)(2,1)}, u32[]{:S(2)}) copy-start(bf16[32,8,16,128]{3,2,1,0:T(8,128)(2,1)} %copy-done.11) | copy-start | bytes 3145732
  390.3 6.2 copy-start.20
  401.0 2.1 copy-start.17
  403.1 383.0 %copy-start.1 = (bf16[1,256,4096]{2,1,0:T(8,128)(2,1)S(1)}, bf16[1,256,4096]{2,1,0:T(8,128)(2,1)}, u32[]{:S(2)}) copy-start(bf16[1,256,4096]{2,1,0:T(8,128)(2,1)} %param.8) | copy-start | bytes 6291460
  (5 other events, 6.0 us)
Sparse Core Ops, SparseCore 0:
  13.6 50.7 all-gather.16
  67.9 48.4 all-gather.8
  120.0 48.7 all-gather.10
  190.4 48.3 all-gather.18
  242.4 48.4 all-gather.12
  293.2 45.5 reduce-scatter.2
  340.5 49.7 all-gather.14
  393.3 392.7 reduce-scatter.4
where the time goes:
time: 793 us
  waiting for transfers between devices  689 us (87%)
  matrix products  40.5 us (5%)
  other arithmetic  27.8 us (4%)
  local copies, waits for them, and re-layouts  20.6 us (3%)
  between operations  14.4 us (2%)
    reduce_scatter x1, waiting for transfers between devices, body(): lax.psum_scatter(half_rows, SEQ, scatter_dimension=0, tiled=True)  381 us
    all_gather x6, waiting for transfers between devices, carried_in(): pieces = lax.all_gather(total, axis)  264 us
    reduce_scatter x1, waiting for transfers between devices, body(): lax.psum_scatter(jnp.einsum('tr,td->rd', attended_rows, cotangent, prefer...  44.3 us
    add x6, other arithmetic, adding(): return earlier + later  26.2 us
    unnamed x49, local copies, waits for them, and re-layouts  16.5 us
  transfers between devices with their start and end apart: 8, of which 8 were waited for; matrix products, arithmetic and copies ran while one was open for 6% of the time, Pallas kernels for 0%

commit v1 on v0

v1 whole, which is shorter than its diff:
```python
import functools

import jax
import jax.numpy as jnp
from jax import lax
from jax.experimental import pallas as pl
from jax.experimental.pallas import tpu as pltpu
from jax.sharding import Mesh
from jax.sharding import PartitionSpec as P

P_SIZE = 128
H = 16
HD = 2048
D = 4096
TOK = 256
EPS = 1e-06
F32 = jnp.float32
BF16 = jnp.bfloat16
MESH = pl.DeviceIdType.MESH
DP = "dp"
SEQ = ("seq_0", "seq_1", "seq_2")
DP_SEQ = (DP,) + SEQ
N_CHUNK = 4
WIDTHS = (1536, 1280, 1280)
STARTS = (0, 1536, 2816)
ORDERS = ((0, 1, 2), (1, 2, 0), (2, 0, 1))
COL = 256
W_ROWS = 256
W_TILES = HD // W_ROWS


def dot_nn(a, b):
    return lax.dot_general(a, b, (((1,), (0,)), ((), ())), preferred_element_type=F32)


def dot_nt(a, b):
    return lax.dot_general(a, b, (((1,), (1,)), ((), ())), preferred_element_type=F32)


def dot_tn(a, b):
    return lax.dot_general(a, b, (((0,), (0,)), ((), ())), preferred_element_type=F32)


def two_parts(x):
    high = x.astype(BF16)
    return high, (x - high.astype(F32)).astype(BF16)


def send(src, dst, send_sem, recv_sem, device):
    return pltpu.make_async_remote_copy(
        src_ref=src, dst_ref=dst, send_sem=send_sem, recv_sem=recv_sem,
        device_id=device, device_id_type=MESH,
    )


class Scan:
    def __init__(self, where, bufs, sems, reverse):
        self.z, self.x, self.y = where
        self.S, self.YR, self.T, self.XR, self.PT, self.ZR, self.XC, self.R = bufs
        self.ss, self.rs = sems
        self.reverse = reverse

    def order(self):
        return range(3, -1, -1) if self.reverse else range(4)

    def copies(self, stage, c):
        out = []
        for r in range(1, 4):
            s, v = self.ss.at[c, stage, r], self.rs.at[c, stage, r]
            yt, xt, zt = (self.y + r) % 4, (self.x + r) % 4, (self.z + r) % 4
            if stage == 0:
                out.append(send(self.S.at[yt, c], self.YR.at[c, self.y], s, v, {SEQ[2]: yt}))
            elif stage == 1:
                out.append(send(self.T.at[c, xt], self.XR.at[c, self.x], s, v, {SEQ[1]: xt}))
            elif stage == 2:
                out.append(send(self.PT.at[c], self.ZR.at[c, self.z], s, v, {SEQ[0]: zt}))
            elif stage == 3:
                out.append(send(self.XR.at[c, xt], self.XC.at[c, self.x], s, v, {SEQ[1]: xt}))
            else:
                out.append(send(self.YR.at[c, yt], self.R.at[self.y, c], s, v, {SEQ[2]: yt}))
        return out

    def landing(self, stage, c):
        for r in range(1, 4):
            s, v = self.ss.at[c, stage, r], self.rs.at[c, stage, r]
            yf, xf, zf = (self.y + 4 - r) % 4, (self.x + 4 - r) % 4, (self.z + 4 - r) % 4
            if stage == 0:
                ref, dev = self.YR.at[c, yf], {SEQ[2]: yf}
            elif stage == 1:
                ref, dev = self.XR.at[c, xf], {SEQ[1]: xf}
            elif stage == 2:
                ref, dev = self.ZR.at[c, zf], {SEQ[0]: zf}
            elif stage == 3:
                ref, dev = self.XC.at[c, xf], {SEQ[1]: xf}
            else:
                ref, dev = self.R.at[yf, c], {SEQ[2]: yf}
            send(ref, ref, s, v, dev).wait_recv()

    def go(self, stage, c):
        for copy in self.copies(stage, c):
            copy.start()

    def step(self, s, c):
        if s > 0:
            self.landing(s - 1, c)
        if s == 0:
            self.YR[c, self.y] = self.S[self.y, c]
        elif s == 1:
            running = None
            for k in self.order():
                now = self.YR[c, k]
                self.YR[c, k] = jnp.zeros_like(now) if running is None else running
                running = now if running is None else running + now
            self.T[c] = running.reshape(4, 32, 128)
            self.XR[c, self.x] = self.T[c, self.x]
        elif s == 2:
            running = None
            for k in self.order():
                now = self.XR[c, k]
                self.XR[c, k] = jnp.zeros_like(now) if running is None else running
                running = now if running is None else running + now
            self.PT[c] = running
            self.ZR[c, self.z] = running
        elif s == 3:
            base = jnp.zeros((32, 128), F32)
            for k in range(4):
                passed = (self.z < k) if self.reverse else (self.z > k)
                base = base + jnp.where(passed, self.ZR[c, k], 0.0)
            for k in range(4):
                self.XR[c, k] = self.XR[c, k] + base
            self.XC[c, self.x] = self.XR[c, self.x]
        elif s == 4:
            carry = self.XC[c].reshape(128, 128)
            for k in range(4):
                self.YR[c, k] = self.YR[c, k] + carry
            self.R[self.y, c] = self.YR[c, self.y]
        if s < 5:
            self.go(s, c)

    def drain(self, stage):
        for c in range(N_CHUNK):
            for copy in self.copies(stage, c):
                copy.wait_send()


class Color:
    def __init__(self, where, order, part, recv, ss, rs):
        self.where, self.order, self.part, self.recv, self.ss, self.rs = where, order, part, recv, ss, rs

    def axis(self, phase):
        return self.order[phase]

    def slot(self, phase, t, u):
        idx = [slice(None)] * 3
        for p in range(phase):
            idx[self.order[p]] = self.where[self.order[p]]
        idx[self.order[phase]] = t
        if phase == 0:
            nxt = self.order[1]
            idx[nxt] = (self.where[nxt] + (2, 1, 3, 0)[u]) % 4
        return idx

    def number(self, phase, kind, u):
        return (kind * 4 + u) if phase == 0 else (24 + 6 * (phase - 1) + kind)

    def copy(self, phase, kind, u=0):
        a = self.axis(phase)
        m = self.where[a]
        up = kind % 2 == 0
        to = (m + 1) % 4 if up else (m + 3) % 4
        t = (m + 2) % 4 if kind < 2 else to
        half = (0, 1, 1, 0, 0, 1)[kind]
        n = self.number(phase, kind, u)
        src = self.part.at[tuple(self.slot(phase, t, u)) + (half,)]
        dst = self.recv[phase].at[kind, u] if phase == 0 else self.recv[phase].at[kind]
        return send(src, dst, self.ss.at[n], self.rs.at[n], {SEQ[a]: to})

    def go(self, phase, kind, u=0):
        self.copy(phase, kind, u).start()

    def got(self, phase, kind, u=0):
        self.copy(phase, kind, u).wait_recv()
        return self.recv[phase][kind, u] if phase == 0 else self.recv[phase][kind]

    def relay(self, phase, u=0):
        m = self.where[self.axis(phase)]
        for kind, to, half in ((0, (m + 1) % 4, 0), (1, (m + 3) % 4, 1)):
            more = self.got(phase, kind, u)
            at = tuple(self.slot(phase, to, u)) + (half,)
            self.part[at] = self.part[at] + more
            self.go(phase, 4 + kind, u)

    def finish(self, phase, u=0):
        m = self.where[self.axis(phase)]
        for half, kinds in ((0, (3, 4)), (1, (2, 5))):
            more = self.got(phase, kinds[0], u) + self.got(phase, kinds[1], u)
            at = tuple(self.slot(phase, m, u)) + (half,)
            self.part[at] = self.part[at] + more

    def drain(self):
        for kind in range(6):
            for u in range(4):
                self.copy(0, kind, u).wait_send()
            for phase in (1, 2):
                self.copy(phase, kind).wait_send()


def kernel(
    q_hbm, k_hbm, v_hbm, og_hbm, w_hbm,
    att_out, qg_out, kg_out, vg_out, wg_out,
    q_v, k_v, v_v, og_v, ogp_v, w_v, grad_v, att_v, do_v, attT, attP, attS, attR,
    state, yr1, t1, xr1, pt1, zr1, xc1, r1,
    yr2, t2, xr2, pt2, zr2, xc2, r2,
    p0, p1, p2, a0, a1, a2, b0, b1, b2, c0, c1, c2,
    in_sem, w_sem, out_sem, s1s, s1r, s2s, s2r, css, crs, ogs, ogr, ats, atr,
):
    d = lax.axis_index(DP)
    where = tuple(lax.axis_index(a) for a in SEQ)
    z, x, y = where
    other = {DP: 1 - d}
    parts = (p0, p1, p2)

    loads = [
        pltpu.make_async_copy(src.at[0], dst, in_sem.at[i])
        for i, (src, dst) in enumerate(((k_hbm, k_v), (v_hbm, v_v), (og_hbm, og_v), (q_hbm, q_v)))
    ]
    for load in loads:
        load.start()

    def w_load(i):
        return pltpu.make_async_copy(
            w_hbm.at[pl.ds(pl.multiple_of(i * W_ROWS, W_ROWS), W_ROWS)], w_v.at[i % 2], w_sem.at[i % 2]
        )

    w_load(0).start()
    w_load(1).start()

    barrier = pltpu.get_barrier_semaphore()
    pl.semaphore_signal(barrier, inc=1, device_id=other, device_id_type=MESH)
    for a in range(3):
        for r in range(1, 4):
            pl.semaphore_signal(barrier, inc=1, device_id={SEQ[a]: (where[a] + r) % 4}, device_id_type=MESH)

    scan1 = Scan(where, (state, yr1, t1, xr1, pt1, zr1, xc1, r1), (s1s, s1r), False)
    scan2 = Scan(where, (state, yr2, t2, xr2, pt2, zr2, xc2, r2), (s2s, s2r), True)
    colors = [
        Color(where, ORDERS[i], parts[i], ((a0, b0, c0), (a1, b1, c1), (a2, b2, c2))[i], css.at[i], crs.at[i])
        for i in range(3)
    ]

    def cols(h):
        return pl.ds(pl.multiple_of(h * P_SIZE, P_SIZE), P_SIZE)

    def states(c):
        def one(j, carry):
            at = cols(4 * j + c)
            state[j, c] = dot_tn(k_v[:, at], v_v[:, at])
            return carry
        lax.fori_loop(0, 4, one, 0)

    loads[0].wait()
    loads[1].wait()
    states(0)
    pl.semaphore_wait(barrier, 10)
    scan1.step(0, 0)
    for c in range(1, N_CHUNK):
        states(c)
        scan1.step(0, c)

    loads[2].wait()

    def og_copy(i):
        return send(parts[i].at[0], parts[i].at[1], ogs.at[i], ogr.at[i], other)

    for i in range(3):
        def put(n, carry, i=i):
            rows = pl.ds(pl.multiple_of(n * 64, 64), 64)
            block = og_v[rows, STARTS[i]:STARTS[i] + WIDTHS[i]].astype(F32)
            parts[i][0, n] = block.reshape(4, 2, 8, WIDTHS[i])
            return carry
        lax.fori_loop(0, 4, put, 0)
        og_copy(i).start()

    def grad_tiles(lo, hi):
        def one(i, carry):
            w_load(i).wait()
            block = dot_nt(og_v[...], w_v[i % 2])
            at = pl.ds(pl.multiple_of(i * W_ROWS, W_ROWS), W_ROWS)
            grad_v[:, at] = block

            @pl.when(i + 2 < W_TILES)
            def _():
                w_load(i + 2).start()
            return carry
        lax.fori_loop(lo, hi, one, 0)

    def og_take(i):
        og_copy(i).wait_recv()
        def take(n, carry):
            rows = pl.ds(pl.multiple_of(n * 64, 64), 64)
            block = parts[i][1, n].reshape(64, WIDTHS[i])
            ogp_v[rows, STARTS[i]:STARTS[i] + WIDTHS[i]] = block.astype(BF16)
            return carry
        lax.fori_loop(0, 4, take, 0)

    lower = (
        lax.broadcasted_iota(jnp.int32, (TOK, TOK), 0) >= lax.broadcasted_iota(jnp.int32, (TOK, TOK), 1)
    )

    def forward_heads(c):
        def one(j, carry):
            h = 4 * j + c
            at = cols(h)
            q, k, v = q_v[:, at], k_v[:, at], v_v[:, at]
            probs = jnp.where(lower, dot_nt(q, k), 0.0).astype(BF16)
            high, low = two_parts(r1[j, c])
            o = dot_nn(probs, v) + (dot_nn(q, high) + dot_nn(q, low))
            inverse = lax.rsqrt(jnp.mean(o * o, axis=-1, keepdims=True) + EPS)
            a = o * inverse
            att = a.astype(BF16)
            att_v[:, at] = att
            turned = att.astype(F32).T.astype(BF16).reshape(2, 4, 16, TOK)
            hh = h % 8
            attT[h // 8, hh // 2, pl.ds(2 * (hh % 2), 2)] = turned
            grad = grad_v[:, at]
            d_o = (inverse * (grad - a * jnp.mean(grad * a, axis=-1, keepdims=True))).astype(BF16)
            do_v[:, at] = d_o
            state[j, c] = dot_tn(q, d_o)
            return carry
        lax.fori_loop(0, 4, one, 0)

    def att_copies(c):
        return [
            send(attS.at[2 * c + i], attR.at[2 * c + i], ats.at[2 * c + i], atr.at[2 * c + i], other)
            for i in range(2)
        ]

    def att_give(c):
        for i, copy in enumerate(att_copies(c)):
            hh = 4 * i + c
            attS[2 * c + i] = attT[1 - d, hh // 2, 2 * (hh % 2):2 * (hh % 2) + 2].astype(F32)
            copy.start()

    def att_take(c):
        for i, copy in enumerate(att_copies(c)):
            hh = 4 * i + c
            copy.wait_recv()
            attP[hh // 2, 2 * (hh % 2):2 * (hh % 2) + 2] = attR[2 * c + i].astype(BF16)

    grad_tiles(0, 4)
    fill = {1: lambda: grad_tiles(4, 6), 2: lambda: grad_tiles(6, 8), 3: lambda: og_take(0),
            4: lambda: og_take(1), 5: lambda: og_take(2)}
    for t in range(1, 5 + N_CHUNK):
        for s in range(5, 0, -1):
            c = t - s
            if 0 <= c < N_CHUNK:
                scan1.step(s, c)
                if s == 5:
                    if c == 0:
                        scan1.drain(0)
                        loads[3].wait()
                    forward_heads(c)
                    scan2.step(0, c)
                    att_give(c)
        if t in fill:
            fill[t]()
    att_save = pltpu.make_async_copy(att_v, att_out.at[0], out_sem.at[0])
    att_save.start()
    for c in range(N_CHUNK):
        att_take(c)
    for i in range(3):
        og_copy(i).wait_send()

    def product(i, offset):
        color = colors[i]
        axis = ORDERS[i][0]
        t = (where[axis] + offset) % 4
        idx = [slice(None)] * 3
        idx[axis] = t
        idx = tuple(idx)
        mine = attT[(d,) + idx].reshape(TOK, TOK)
        theirs = attP[idx].reshape(TOK, TOK)

        def one(n, carry):
            at = pl.ds(pl.multiple_of(STARTS[i] + n * COL, COL), COL)
            block = dot_nn(mine, og_v[:, at]) + dot_nn(theirs, ogp_v[:, at])
            to = pl.ds(pl.multiple_of(n * COL, COL), COL)
            color.part[idx + (slice(None), slice(None), to)] = block.reshape(4, 4, 2, 8, COL)
            return carry
        lax.fori_loop(0, WIDTHS[i] // COL, one, 0)

    def backward_heads(c):
        def one(j, carry):
            at = cols(4 * j + c)
            q, k, v, d_o = q_v[:, at], k_v[:, at], v_v[:, at], do_v[:, at]
            probs = jnp.where(lower, dot_nt(q, k), 0.0).astype(BF16)
            d_probs = jnp.where(lower, dot_nt(d_o, v), 0.0).astype(BF16)
            high, low = two_parts(r1[j, c])
            q_grad = dot_nn(d_probs, k) + (dot_nt(d_o, high) + dot_nt(d_o, low))
            high, low = two_parts(r2[j, c])
            k_grad = dot_tn(d_probs, q) + (dot_nt(v, high) + dot_nt(v, low))
            v_grad = dot_tn(probs, d_o) + (dot_nn(k, high) + dot_nn(k, low))
            q_v[:, at] = q_grad.astype(BF16)
            k_v[:, at] = k_grad.astype(BF16)
            v_v[:, at] = v_grad.astype(BF16)
            return carry
        lax.fori_loop(0, 4, one, 0)

    for i in range(3):
        product(i, 2)
        for u in range(4):
            colors[i].go(0, 0, u)
            colors[i].go(0, 1, u)
    for i in range(3):
        product(i, 1)
        for u in range(4):
            colors[i].go(0, 2, u)
    for i in range(3):
        product(i, 3)
        for u in range(4):
            colors[i].go(0, 3, u)
    for i in range(3):
        product(i, 0)

    for t in range(1, 5 + N_CHUNK):
        for s in range(5, 0, -1):
            c = t - s
            if 0 <= c < N_CHUNK:
                scan2.step(s, c)
                if s == 5:
                    backward_heads(c)
        if t <= 4:
            for color in colors:
                color.relay(0, t - 1)
    saves = [
        pltpu.make_async_copy(src, dst.at[0], out_sem.at[1 + i])
        for i, (src, dst) in enumerate(((q_v, qg_out), (k_v, kg_out), (v_v, vg_out)))
    ]
    for save in saves:
        save.start()

    for u in range(4):
        for color in colors:
            color.finish(0, u)
            if u == 0:
                color.go(1, 0)
                color.go(1, 1)
            elif u == 1:
                color.go(1, 2)
            elif u == 2:
                color.go(1, 3)
    for color in colors:
        color.relay(1)
    for color in colors:
        color.finish(1)
        for kind in range(4):
            color.go(2, kind)
    for color in colors:
        color.relay(2)
    outs = []
    for i, color in enumerate(colors):
        color.finish(2)
        out = pltpu.make_async_copy(
            color.part.at[z, x, y],
            wg_out.at[:, :, STARTS[i]:STARTS[i] + WIDTHS[i]],
            out_sem.at[4 + i],
        )
        out.start()
        outs.append(out)

    for stage in range(1, 5):
        scan1.drain(stage)
    for stage in range(5):
        scan2.drain(stage)
    for color in colors:
        color.drain()
    for c in range(N_CHUNK):
        for copy in att_copies(c):
            copy.wait_send()
    att_save.wait()
    for save in saves:
        save.wait()
    for out in outs:
        out.wait()


def body(queries, keys, values, out_grad, out_weight):
    vm = pltpu.VMEM
    dma = pltpu.SemaphoreType.DMA
    flat = jax.ShapeDtypeStruct((1, TOK, HD), BF16)

    def scan_bufs():
        return [
            vm((4, 4, 128, 128), F32), vm((4, 4, 32, 128), F32), vm((4, 4, 32, 128), F32),
            vm((4, 32, 128), F32), vm((4, 4, 32, 128), F32), vm((4, 4, 32, 128), F32),
            vm((4, 4, 128, 128), F32),
        ]

    scratch = [
        vm((TOK, HD), BF16), vm((TOK, HD), BF16), vm((TOK, HD), BF16),
        vm((TOK, D), BF16), vm((TOK, D), BF16), vm((2, W_ROWS, D), BF16),
        vm((TOK, HD), F32), vm((TOK, HD), BF16), vm((TOK, HD), BF16),
        vm((2, 4, 4, 4, 16, TOK), BF16), vm((4, 4, 4, 16, TOK), BF16),
        vm((8, 2, 4, 16, TOK), F32), vm((8, 2, 4, 16, TOK), F32),
        vm((4, 4, 128, 128), F32),
        *scan_bufs(), *scan_bufs(),
        *[vm((4, 4, 4, 2, 8, w), F32) for w in WIDTHS],
    ]
    scratch += [vm((6, 4, 4, 8, w), F32) for w in WIDTHS]
    scratch += [vm((6, 4, 8, w), F32) for w in WIDTHS]
    scratch += [vm((6, 8, w), F32) for w in WIDTHS]
    scratch += [
        dma((4,)), dma((2,)), dma((7,)),
        dma((4, 5, 4)), dma((4, 5, 4)), dma((4, 5, 4)), dma((4, 5, 4)),
        dma((3, 36)), dma((3, 36)), dma((3,)), dma((3,)), dma((8,)), dma((8,)),
    ]
    any_space = pl.BlockSpec(memory_space=pl.ANY)
    attended, d_query, d_key, d_value, weight_grad = pl.pallas_call(
        kernel,
        out_shape=(flat, flat, flat, flat, jax.ShapeDtypeStruct((2, 8, D), F32)),
        in_specs=[any_space] * 5,
        out_specs=(any_space,) * 5,
        scratch_shapes=scratch,
        compiler_params=pltpu.CompilerParams(
            collective_id=0, has_side_effects=True, vmem_limit_bytes=66_900_000
        ),
        name="block",
    )(queries, keys, values, out_grad, out_weight)
    return attended, d_query, d_key, d_value, weight_grad.reshape(16, D)


def solution(mesh):
    split = Mesh(mesh.devices.reshape(mesh.shape[DP], 4, 4, 4), DP_SEQ)
    rows = P(DP, SEQ, None)
    return jax.shard_map(
        body, mesh=split, in_specs=(rows, rows, rows, rows, P()),
        out_specs=(rows, rows, rows, rows, P(DP_SEQ, None)), check_vma=False,
    )
```

time: 793 us -> 178 us (0.22)
  waiting for transfers between devices: 689 us -> 0 us
  Pallas kernels: 0 us -> 166 us
  matrix products: 40.5 us -> 0 us
  other arithmetic: 27.8 us -> 0 us
  between operations: 14.4 us -> 0.64 us
  local copies, waits for them, and re-layouts: 20.6 us -> 10.9 us
    reduce_scatter x2 -> x0, waiting for transfers between devices: 425 us -> none  [the longest x1 381 us: body(): lax.psum_scatter(half_rows, SEQ, scatter_dimension=0, tiled=True)]
    all_gather x6 -> x0, waiting for transfers between devices: 264 us -> none  [carried_in(): pieces = lax.all_gather(total, axis)]
    pallas_call x0 -> x1, Pallas kernels: none -> 166 us  [body(): pl.pallas_call(kernel, out_shape=(flat, flat, flat, flat, jax.ShapeDtypeS...]
    dot_general x14 -> x0, matrix products: 40.5 us -> none  [the longest x1 15.3 us: body(): jnp.einsum('tr,td->rd', attended_rows, cotangent, preferred_element_type=...]
    add x6 -> x0, other arithmetic: 26.2 us -> none  [adding(): return earlier + later]
    unnamed x49 -> x5, local copies, waits for them, and re-layouts: 16.5 us -> 10.9 us
  transfers between devices with their start and end apart: 8 -> 0, of which waited for: 8 -> 0; matrix products, arithmetic and copies ran while one was open for 6% -> 0% of each run, Pallas kernels for 0% -> 0%
where the time goes in v1:
time: 178 us; the launch traced here: 177 us
  Pallas kernels  166 us (93%)
  local copies, waits for them, and re-layouts  10.9 us (6%)
    pallas_call x1, Pallas kernels, body(): pl.pallas_call(kernel, out_shape=(flat, flat, flat, flat, jax.ShapeDtypeS...  166 us
    unnamed x5, local copies, waits for them, and re-layouts  10.9 us

profile of v1, /device:TPU:0, one launch (start us, length us, event | category | flops | bytes accessed | tf_op | source)
XLA Modules:
  0.0 177.2 jit_solution(5248373269880200261)
XLA Ops:
  0.6 165.7 %block.1 = (bf16[1,256,2048]{2,1,0:T(8,128)(2,1)}, bf16[1,256,2048]{2,1,0:T(8,128)(2,1)}, bf16[1,256,2048]{2,1,0:T(8,128)(2,1)}, bf16[1,256,2048]{2,1,0:T(8,128)(2,1)}, f32[2,8,4096]{2,1,0:T(8,128)}) custom-call(bf16[1,256,2048]{2,1,0:T(8,128)(2,1)} %q_hbm.1, bf16[1,256,2048]{2,1,0:T(8,128)(2,1)} %k_hbm.1, bf16[1,256,2048]{2,1,0:T(8,128)(2,1)} %v_hbm.1, ...), custom_call_target="tpu_custom_call" | custom-call | tf_op jit(solution)/shard_map/block/pallas_call | solution.py:518
  166.3 2.3 %copy.15 = bf16[1,256,2048]{2,1,0:T(8,128)(2,1)} copy(bf16[1,256,2048]{2,1,0:T(8,128)(2,1)} %get-tuple-element.20) | data formatting | bytes 2097152
  168.6 2.3 %copy.16 = bf16[1,256,2048]{2,1,0:T(8,128)(2,1)} copy(bf16[1,256,2048]{2,1,0:T(8,128)(2,1)} %get-tuple-element.21) | data formatting | bytes 2097152
  170.9 2.3 %copy.17 = bf16[1,256,2048]{2,1,0:T(8,128)(2,1)} copy(bf16[1,256,2048]{2,1,0:T(8,128)(2,1)} %get-tuple-element.22) | data formatting | bytes 2097152
  173.2 2.3 %copy.18 = bf16[1,256,2048]{2,1,0:T(8,128)(2,1)} copy(bf16[1,256,2048]{2,1,0:T(8,128)(2,1)} %get-tuple-element.23) | data formatting | bytes 2097152
  175.5 1.7 copy.19

commit v2 on v1

--- a/solution.py
+++ b/solution.py
@@ -27,6 +27,7 @@
 COL = 256
 W_ROWS = 256
 W_TILES = HD // W_ROWS
+VMEM_LIMIT = 62_000_000
 
 
 def dot_nn(a, b):
@@ -51,6 +52,14 @@
         src_ref=src, dst_ref=dst, send_sem=send_sem, recv_sem=recv_sem,
         device_id=device, device_id_type=MESH,
     )
+
+
+def scoped(f):
+    @functools.wraps(f)
+    def named(*args):
+        with jax.named_scope(f.__name__ + "_" + "".join(map(str, args))):
+            return f(*args)
+    return named
 
 
 class Scan:
@@ -101,6 +110,10 @@
             copy.start()
 
     def step(self, s, c):
+        with jax.named_scope(f"scan{int(self.reverse)}_{s}{c}"):
+            self.step_in(s, c)
+
+    def step_in(self, s, c):
         if s > 0:
             self.landing(s - 1, c)
         if s == 0:
@@ -146,6 +159,7 @@
 class Color:
     def __init__(self, where, order, part, recv, ss, rs):
         self.where, self.order, self.part, self.recv, self.ss, self.rs = where, order, part, recv, ss, rs
+        self.gone = set()
 
     def axis(self, phase):
         return self.order[phase]
@@ -178,11 +192,20 @@
     def go(self, phase, kind, u=0):
         self.copy(phase, kind, u).start()
 
+    def left(self, phase, kind, u=0):
+        if (phase, kind, u) not in self.gone:
+            self.gone.add((phase, kind, u))
+            self.copy(phase, kind, u).wait_send()
+
     def got(self, phase, kind, u=0):
         self.copy(phase, kind, u).wait_recv()
         return self.recv[phase][kind, u] if phase == 0 else self.recv[phase][kind]
 
     def relay(self, phase, u=0):
+        with jax.named_scope(f"relay{self.order[0]}_{phase}{u}"):
+            self.relay_in(phase, u)
+
+    def relay_in(self, phase, u=0):
         m = self.where[self.axis(phase)]
         for kind, to, half in ((0, (m + 1) % 4, 0), (1, (m + 3) % 4, 1)):
             more = self.got(phase, kind, u)
@@ -190,29 +213,37 @@
             self.part[at] = self.part[at] + more
             self.go(phase, 4 + kind, u)
 
-    def finish(self, phase, u=0):
+    def finish(self, phase, u=0, to=None):
+        with jax.named_scope(f"finish{self.order[0]}_{phase}{u}"):
+            self.finish_in(phase, u, to)
+
+    def finish_in(self, phase, u=0, to=None):
         m = self.where[self.axis(phase)]
         for half, kinds in ((0, (3, 4)), (1, (2, 5))):
             more = self.got(phase, kinds[0], u) + self.got(phase, kinds[1], u)
             at = tuple(self.slot(phase, m, u)) + (half,)
-            self.part[at] = self.part[at] + more
+            if to is None:
+                self.part[at] = self.part[at] + more
+            else:
+                out, start, width = to
+                out[half, :, start:start + width] = self.part[at] + more
 
     def drain(self):
         for kind in range(6):
             for u in range(4):
-                self.copy(0, kind, u).wait_send()
+                self.left(0, kind, u)
             for phase in (1, 2):
-                self.copy(phase, kind).wait_send()
+                self.left(phase, kind)
 
 
 def kernel(
     q_hbm, k_hbm, v_hbm, og_hbm, w_hbm,
-    att_out, qg_out, kg_out, vg_out, wg_out,
-    q_v, k_v, v_v, og_v, ogp_v, w_v, grad_v, att_v, do_v, attT, attP, attS, attR,
+    att_v, q_v, k_v, v_v, wg_v,
+    og_v, w_v, grad_v, intra_v, do_v, attT, attP, attS, attR,
     state, yr1, t1, xr1, pt1, zr1, xc1, r1,
     yr2, t2, xr2, pt2, zr2, xc2, r2,
     p0, p1, p2, a0, a1, a2, b0, b1, b2, c0, c1, c2,
-    in_sem, w_sem, out_sem, s1s, s1r, s2s, s2r, css, crs, ogs, ogr, ats, atr,
+    in_sem, w_sem, s1s, s1r, s2s, s2r, css, crs, ogs, ogr, ats, atr,
 ):
     d = lax.axis_index(DP)
     where = tuple(lax.axis_index(a) for a in SEQ)
@@ -222,7 +253,7 @@
 
     loads = [
         pltpu.make_async_copy(src.at[0], dst, in_sem.at[i])
-        for i, (src, dst) in enumerate(((k_hbm, k_v), (v_hbm, v_v), (og_hbm, og_v), (q_hbm, q_v)))
+        for i, (src, dst) in enumerate(((k_hbm, k_v), (v_hbm, v_v), (og_hbm, og_v.at[:TOK]), (q_hbm, q_v)))
     ]
     for load in loads:
         load.start()
@@ -251,17 +282,27 @@
     def cols(h):
         return pl.ds(pl.multiple_of(h * P_SIZE, P_SIZE), P_SIZE)
 
+    def heads_of(fn, c, width=2):
+        def one(n, carry):
+            fn([n * width + i for i in range(width)], c)
+            return carry
+        lax.fori_loop(0, 4 // width, one, 0)
+
+    @scoped
     def states(c):
-        def one(j, carry):
-            at = cols(4 * j + c)
-            state[j, c] = dot_tn(k_v[:, at], v_v[:, at])
-            return carry
-        lax.fori_loop(0, 4, one, 0)
-
-    loads[0].wait()
-    loads[1].wait()
+        def some(js, c):
+            at = [cols(4 * j + c) for j in js]
+            out = [dot_tn(k_v[:, a], v_v[:, a]) for a in at]
+            for j, value in zip(js, out):
+                state[j, c] = value
+        heads_of(some, c)
+
+    with jax.named_scope("load"):
+        loads[0].wait()
+        loads[1].wait()
     states(0)
-    pl.semaphore_wait(barrier, 10)
+    with jax.named_scope("enter"):
+        pl.semaphore_wait(barrier, 10)
     scan1.step(0, 0)
     for c in range(1, N_CHUNK):
         states(c)
@@ -281,10 +322,11 @@
         lax.fori_loop(0, 4, put, 0)
         og_copy(i).start()
 
+    @scoped
     def grad_tiles(lo, hi):
         def one(i, carry):
             w_load(i).wait()
-            block = dot_nt(og_v[...], w_v[i % 2])
+            block = dot_nt(og_v[:TOK], w_v[i % 2])
             at = pl.ds(pl.multiple_of(i * W_ROWS, W_ROWS), W_ROWS)
             grad_v[:, at] = block
 
@@ -294,12 +336,13 @@
             return carry
         lax.fori_loop(lo, hi, one, 0)
 
+    @scoped
     def og_take(i):
         og_copy(i).wait_recv()
         def take(n, carry):
-            rows = pl.ds(pl.multiple_of(n * 64, 64), 64)
+            rows = pl.ds(pl.multiple_of(TOK + n * 64, 64), 64)
             block = parts[i][1, n].reshape(64, WIDTHS[i])
-            ogp_v[rows, STARTS[i]:STARTS[i] + WIDTHS[i]] = block.astype(BF16)
+            og_v[rows, STARTS[i]:STARTS[i] + WIDTHS[i]] = block.astype(BF16)
             return carry
         lax.fori_loop(0, 4, take, 0)
 
@@ -307,27 +350,41 @@
         lax.broadcasted_iota(jnp.int32, (TOK, TOK), 0) >= lax.broadcasted_iota(jnp.int32, (TOK, TOK), 1)
     )
 
+    @scoped
+    def inside_heads(c):
+        def some(js, c):
+            at = [cols(4 * j + c) for j in js]
+            scores = [dot_nt(q_v[:, a], k_v[:, a]) for a in at]
+            probs = [jnp.where(lower, x, 0.0).astype(BF16) for x in scores]
+            out = [dot_nn(p, v_v[:, a]) for p, a in zip(probs, at)]
+            for a, value in zip(at, out):
+                intra_v[:, a] = value
+        heads_of(some, c)
+
+    @scoped
     def forward_heads(c):
-        def one(j, carry):
-            h = 4 * j + c
-            at = cols(h)
-            q, k, v = q_v[:, at], k_v[:, at], v_v[:, at]
-            probs = jnp.where(lower, dot_nt(q, k), 0.0).astype(BF16)
-            high, low = two_parts(r1[j, c])
-            o = dot_nn(probs, v) + (dot_nn(q, high) + dot_nn(q, low))
-            inverse = lax.rsqrt(jnp.mean(o * o, axis=-1, keepdims=True) + EPS)
-            a = o * inverse
-            att = a.astype(BF16)
-            att_v[:, at] = att
-            turned = att.astype(F32).T.astype(BF16).reshape(2, 4, 16, TOK)
-            hh = h % 8
-            attT[h // 8, hh // 2, pl.ds(2 * (hh % 2), 2)] = turned
-            grad = grad_v[:, at]
-            d_o = (inverse * (grad - a * jnp.mean(grad * a, axis=-1, keepdims=True))).astype(BF16)
-            do_v[:, at] = d_o
-            state[j, c] = dot_tn(q, d_o)
-            return carry
-        lax.fori_loop(0, 4, one, 0)
+        def some(js, c):
+            at = [cols(4 * j + c) for j in js]
+            q = [q_v[:, a] for a in at]
+            split = [two_parts(r1[j, c]) for j in js]
+            inter = [dot_nn(a, high) + dot_nn(a, low) for a, (high, low) in zip(q, split)]
+            o = [intra_v[:, a] + x for a, x in zip(at, inter)]
+            inverse = [lax.rsqrt(jnp.mean(x * x, axis=-1, keepdims=True) + EPS) for x in o]
+            normed = [x * i for x, i in zip(o, inverse)]
+            grad = [grad_v[:, a] for a in at]
+            level = [jnp.mean(g * n, axis=-1, keepdims=True) for g, n in zip(grad, normed)]
+            d_o = [(i * (g - n * m)).astype(BF16) for i, g, n, m in zip(inverse, grad, normed, level)]
+            d_prefix = [dot_tn(a, b) for a, b in zip(q, d_o)]
+            att = [n.astype(BF16) for n in normed]
+            turned = [a.astype(F32).T.astype(BF16).reshape(2, 4, 16, TOK) for a in att]
+            for i, j in enumerate(js):
+                h = 4 * j + c
+                hh = h % 8
+                att_v[:, at[i]] = att[i]
+                do_v[:, at[i]] = d_o[i]
+                state[j, c] = d_prefix[i]
+                attT[h // 8, hh // 2, pl.ds(2 * (hh % 2), 2)] = turned[i]
+        heads_of(some, c)
 
     def att_copies(c):
         return [
@@ -335,42 +392,46 @@
             for i in range(2)
         ]
 
+    @scoped
     def att_give(c):
         for i, copy in enumerate(att_copies(c)):
             hh = 4 * i + c
             attS[2 * c + i] = attT[1 - d, hh // 2, 2 * (hh % 2):2 * (hh % 2) + 2].astype(F32)
             copy.start()
 
+    @scoped
     def att_take(c):
         for i, copy in enumerate(att_copies(c)):
             hh = 4 * i + c
             copy.wait_recv()
             attP[hh // 2, 2 * (hh % 2):2 * (hh % 2) + 2] = attR[2 * c + i].astype(BF16)
 
-    grad_tiles(0, 4)
-    fill = {1: lambda: grad_tiles(4, 6), 2: lambda: grad_tiles(6, 8), 3: lambda: og_take(0),
-            4: lambda: og_take(1), 5: lambda: og_take(2)}
-    for t in range(1, 5 + N_CHUNK):
-        for s in range(5, 0, -1):
-            c = t - s
-            if 0 <= c < N_CHUNK:
-                scan1.step(s, c)
-                if s == 5:
-                    if c == 0:
-                        scan1.drain(0)
-                        loads[3].wait()
-                    forward_heads(c)
-                    scan2.step(0, c)
-                    att_give(c)
-        if t in fill:
-            fill[t]()
-    att_save = pltpu.make_async_copy(att_v, att_out.at[0], out_sem.at[0])
-    att_save.start()
+    forward = (
+        (grad_tiles, 0, 4), (1, 0), (grad_tiles, 4, 6), (1, 1), (grad_tiles, 6, 8), (2, 0), (1, 2),
+        (inside_heads, 0), (2, 1), (1, 3), (inside_heads, 1), (3, 0), (2, 2), (og_take, 0), (inside_heads, 2),
+        (3, 1), (2, 3), (4, 0), (inside_heads, 3), (3, 2), (4, 1), (3, 3), (og_take, 1), (4, 2), (og_take, 2),
+        (4, 3),
+    )
+    loads[3].wait()
+    for item in forward:
+        if callable(item[0]):
+            item[0](*item[1:])
+        else:
+            scan1.step(*item)
+    scan1.drain(0)
+    for c in range(N_CHUNK):
+        scan1.step(5, c)
+        forward_heads(c)
+        scan2.step(0, c)
+        att_give(c)
+        if c >= 2:
+            scan2.step(1, c - 2)
     for c in range(N_CHUNK):
         att_take(c)
     for i in range(3):
         og_copy(i).wait_send()
 
+    @scoped
     def product(i, offset):
         color = colors[i]
         axis = ORDERS[i][0]
@@ -378,77 +439,102 @@
         idx = [slice(None)] * 3
         idx[axis] = t
         idx = tuple(idx)
-        mine = attT[(d,) + idx].reshape(TOK, TOK)
-        theirs = attP[idx].reshape(TOK, TOK)
-
-        def one(n, carry):
-            at = pl.ds(pl.multiple_of(STARTS[i] + n * COL, COL), COL)
-            block = dot_nn(mine, og_v[:, at]) + dot_nn(theirs, ogp_v[:, at])
-            to = pl.ds(pl.multiple_of(n * COL, COL), COL)
-            color.part[idx + (slice(None), slice(None), to)] = block.reshape(4, 4, 2, 8, COL)
-            return carry
-        lax.fori_loop(0, WIDTHS[i] // COL, one, 0)
-
+        both = jnp.concatenate([attT[(d,) + idx].reshape(TOK, TOK), attP[idx].reshape(TOK, TOK)], axis=1)
+        for n in range(WIDTHS[i] // COL):
+            at = STARTS[i] + n * COL
+            block = dot_nn(both, og_v[:, at:at + COL])
+            color.part[idx + (slice(None), slice(None), slice(n * COL, (n + 1) * COL))] = block.reshape(4, 4, 2, 8, COL)
+
+    @scoped
     def backward_heads(c):
-        def one(j, carry):
-            at = cols(4 * j + c)
-            q, k, v, d_o = q_v[:, at], k_v[:, at], v_v[:, at], do_v[:, at]
-            probs = jnp.where(lower, dot_nt(q, k), 0.0).astype(BF16)
-            d_probs = jnp.where(lower, dot_nt(d_o, v), 0.0).astype(BF16)
-            high, low = two_parts(r1[j, c])
-            q_grad = dot_nn(d_probs, k) + (dot_nt(d_o, high) + dot_nt(d_o, low))
-            high, low = two_parts(r2[j, c])
-            k_grad = dot_tn(d_probs, q) + (dot_nt(v, high) + dot_nt(v, low))
-            v_grad = dot_tn(probs, d_o) + (dot_nn(k, high) + dot_nn(k, low))
-            q_v[:, at] = q_grad.astype(BF16)
-            k_v[:, at] = k_grad.astype(BF16)
-            v_v[:, at] = v_grad.astype(BF16)
-            return carry
-        lax.fori_loop(0, 4, one, 0)
+        def some(js, c):
+            at = [cols(4 * j + c) for j in js]
+            q, k, v, d_o = ([ref[:, a] for a in at] for ref in (q_v, k_v, v_v, do_v))
+            probs = [jnp.where(lower, dot_nt(a, b), 0.0).astype(BF16) for a, b in zip(q, k)]
+            d_probs = [jnp.where(lower, dot_nt(a, b), 0.0).astype(BF16) for a, b in zip(d_o, v)]
+            before = [two_parts(r1[j, c]) for j in js]
+            after = [two_parts(r2[j, c]) for j in js]
+            n = range(len(js))
+            q_grad = [dot_nn(d_probs[i], k[i]) + sum(dot_nt(d_o[i], p) for p in before[i]) for i in n]
+            k_grad = [dot_tn(d_probs[i], q[i]) + sum(dot_nt(v[i], p) for p in after[i]) for i in n]
+            v_grad = [dot_tn(probs[i], d_o[i]) + sum(dot_nn(k[i], p) for p in after[i]) for i in n]
+            for i in n:
+                q_v[:, at[i]] = q_grad[i].astype(BF16)
+                k_v[:, at[i]] = k_grad[i].astype(BF16)
+                v_v[:, at[i]] = v_grad[i].astype(BF16)
+        heads_of(some, c)
+
+    cz, cx, cy = colors
+
+    def up_down(color, pair, u):
+        color.go(0, 2 * pair, u)
+        color.go(0, 2 * pair + 1, u)
+
+    def paced(color, pair, u):
+        n = 4 * pair + u - 2
+        for up in range(2):
+            color.left(0, 2 * (n // 4) + up, n % 4)
+        up_down(color, pair, u)
 
     for i in range(3):
         product(i, 2)
-        for u in range(4):
-            colors[i].go(0, 0, u)
-            colors[i].go(0, 1, u)
-    for i in range(3):
-        product(i, 1)
-        for u in range(4):
-            colors[i].go(0, 2, u)
-    for i in range(3):
-        product(i, 3)
-        for u in range(4):
-            colors[i].go(0, 3, u)
-    for i in range(3):
-        product(i, 0)
-
-    for t in range(1, 5 + N_CHUNK):
-        for s in range(5, 0, -1):
-            c = t - s
-            if 0 <= c < N_CHUNK:
-                scan2.step(s, c)
-                if s == 5:
-                    backward_heads(c)
-        if t <= 4:
-            for color in colors:
-                color.relay(0, t - 1)
-    saves = [
-        pltpu.make_async_copy(src, dst.at[0], out_sem.at[1 + i])
-        for i, (src, dst) in enumerate(((q_v, qg_out), (k_v, kg_out), (v_v, vg_out)))
-    ]
-    for save in saves:
-        save.start()
-
+        up_down(colors[i], 0, 0)
+        up_down(colors[i], 0, 1)
+    for offset in (1, 3, 0):
+        for i in range(3):
+            product(i, offset)
+    for item in ((1, 2), (1, 3), (2, 0), (2, 1)):
+        scan2.step(*item)
+    for color in colors:
+        paced(color, 0, 2)
+    for item in ((2, 2), (3, 0)):
+        scan2.step(*item)
+    for color in colors:
+        paced(color, 0, 3)
+    for item in ((2, 3), (3, 1)):
+        scan2.step(*item)
     for u in range(4):
-        for color in colors:
-            color.finish(0, u)
-            if u == 0:
-                color.go(1, 0)
-                color.go(1, 1)
-            elif u == 1:
-                color.go(1, 2)
-            elif u == 2:
-                color.go(1, 3)
+        up_down(cz, 1, u)
+    paced(cx, 1, 0)
+    paced(cy, 1, 0)
+    for item in ((4, 0), (3, 2)):
+        scan2.step(*item)
+    cz.relay(0, 0)
+    paced(cx, 1, 1)
+    paced(cy, 1, 1)
+    cz.relay(0, 1)
+    cz.relay(0, 2)
+    for item in ((4, 1), (3, 3)):
+        scan2.step(*item)
+    up_down(cx, 1, 2)
+    up_down(cx, 1, 3)
+    paced(cy, 1, 2)
+    cz.relay(0, 3)
+    for u in range(4):
+        cx.relay(0, u)
+    scan2.step(4, 2)
+    paced(cy, 1, 3)
+    scan2.step(4, 3)
+    for u in range(4):
+        cy.relay(0, u)
+
+    def finish_first(color, u):
+        color.finish(0, u)
+        if u == 0:
+            color.go(1, 0)
+            color.go(1, 1)
+        elif u == 1:
+            color.go(1, 2)
+        elif u == 2:
+            color.go(1, 3)
+
+    for u in range(4):
+        scan2.step(5, u)
+        backward_heads(u)
+        finish_first(cz, u)
+        finish_first(cx, u)
+    for u in range(4):
+        finish_first(cy, u)
     for color in colors:
         color.relay(1)
     for color in colors:
@@ -457,16 +543,8 @@
             color.go(2, kind)
     for color in colors:
         color.relay(2)
-    outs = []
     for i, color in enumerate(colors):
-        color.finish(2)
-        out = pltpu.make_async_copy(
-            color.part.at[z, x, y],
-            wg_out.at[:, :, STARTS[i]:STARTS[i] + WIDTHS[i]],
-            out_sem.at[4 + i],
-        )
-        out.start()
-        outs.append(out)
+        color.finish(2, to=(wg_v, STARTS[i], WIDTHS[i]))
 
     for stage in range(1, 5):
         scan1.drain(stage)
@@ -477,17 +555,23 @@
     for c in range(N_CHUNK):
         for copy in att_copies(c):
             copy.wait_send()
-    att_save.wait()
-    for save in saves:
-        save.wait()
-    for out in outs:
-        out.wait()
+
+
+def store_kernel(*refs):
+    sources, targets, sems = refs[:5], refs[5:10], refs[10]
+    copies = [
+        pltpu.make_async_copy(src, dst.at[0] if i < 4 else dst, sems.at[i])
+        for i, (src, dst) in enumerate(zip(sources, targets))
+    ]
+    for copy in copies:
+        copy.start()
+    for copy in copies:
+        copy.wait()
 
 
 def body(queries, keys, values, out_grad, out_weight):
     vm = pltpu.VMEM
     dma = pltpu.SemaphoreType.DMA
-    flat = jax.ShapeDtypeStruct((1, TOK, HD), BF16)
 
     def scan_bufs():
         return [
@@ -497,9 +581,8 @@
         ]
 
     scratch = [
-        vm((TOK, HD), BF16), vm((TOK, HD), BF16), vm((TOK, HD), BF16),
-        vm((TOK, D), BF16), vm((TOK, D), BF16), vm((2, W_ROWS, D), BF16),
-        vm((TOK, HD), F32), vm((TOK, HD), BF16), vm((TOK, HD), BF16),
+        vm((2 * TOK, D), BF16), vm((2, W_ROWS, D), BF16),
+        vm((TOK, HD), F32), vm((TOK, HD), F32), vm((TOK, HD), BF16),
         vm((2, 4, 4, 4, 16, TOK), BF16), vm((4, 4, 4, 16, TOK), BF16),
         vm((8, 2, 4, 16, TOK), F32), vm((8, 2, 4, 16, TOK), F32),
         vm((4, 4, 128, 128), F32),
@@ -510,22 +593,33 @@
     scratch += [vm((6, 4, 8, w), F32) for w in WIDTHS]
     scratch += [vm((6, 8, w), F32) for w in WIDTHS]
     scratch += [
-        dma((4,)), dma((2,)), dma((7,)),
+        dma((4,)), dma((2,)),
         dma((4, 5, 4)), dma((4, 5, 4)), dma((4, 5, 4)), dma((4, 5, 4)),
         dma((3, 36)), dma((3, 36)), dma((3,)), dma((3,)), dma((8,)), dma((8,)),
     ]
     any_space = pl.BlockSpec(memory_space=pl.ANY)
-    attended, d_query, d_key, d_value, weight_grad = pl.pallas_call(
+    in_vmem = pl.BlockSpec(memory_space=vm)
+    results = pl.pallas_call(
         kernel,
-        out_shape=(flat, flat, flat, flat, jax.ShapeDtypeStruct((2, 8, D), F32)),
+        out_shape=(vm((TOK, HD), BF16),) * 4 + (vm((2, 8, D), F32),),
         in_specs=[any_space] * 5,
-        out_specs=(any_space,) * 5,
+        out_specs=(in_vmem,) * 5,
         scratch_shapes=scratch,
         compiler_params=pltpu.CompilerParams(
-            collective_id=0, has_side_effects=True, vmem_limit_bytes=66_900_000
+            collective_id=0, has_side_effects=True, vmem_limit_bytes=VMEM_LIMIT
         ),
         name="block",
     )(queries, keys, values, out_grad, out_weight)
+    flat = jax.ShapeDtypeStruct((1, TOK, HD), BF16)
+    attended, d_query, d_key, d_value, weight_grad = pl.pallas_call(
+        store_kernel,
+        out_shape=(flat,) * 4 + (jax.ShapeDtypeStruct((2, 8, D), F32),),
+        in_specs=[in_vmem] * 5,
+        out_specs=(any_space,) * 5,
+        scratch_shapes=[dma((5,))],
+        compiler_params=pltpu.CompilerParams(vmem_limit_bytes=1 << 20),
+        name="store",
+    )(*results)
     return attended, d_query, d_key, d_value, weight_grad.reshape(16, D)
 
 

time: 178 us -> 130 us (0.73)
  Pallas kernels: 166 us -> 129 us
  local copies, waits for them, and re-layouts: 10.9 us -> 0 us
    pallas_call x1 -> x2, Pallas kernels: 166 us -> 129 us  [the longest x1 126 us: body(): pl.pallas_call(kernel, out_shape=(vm((TOK, HD), BF16),) * 4 + (vm((2, 8,...]
    unnamed x5 -> x0, local copies, waits for them, and re-layouts: 10.9 us -> none
where the time goes in v2:
time: 130 us; the launch traced here: 129 us
  Pallas kernels  129 us (99%)
    pallas_call x1, Pallas kernels, body(): pl.pallas_call(kernel, out_shape=(vm((TOK, HD), BF16),) * 4 + (vm((2, 8,...  126 us

profile of v2, /device:TPU:0, one launch (start us, length us, event | category | flops | bytes accessed | tf_op | source)
XLA Modules:
  0.0 129.4 jit_solution(5181986378989433228)
XLA Ops:
  0.6 126.5 %block.1 = (bf16[256,2048]{1,0:T(8,128)(2,1)S(1)}, bf16[256,2048]{1,0:T(8,128)(2,1)S(1)}, bf16[256,2048]{1,0:T(8,128)(2,1)S(1)}, bf16[256,2048]{1,0:T(8,128)(2,1)S(1)}, f32[2,8,4096]{2,1,0:T(8,128)S(1)}) custom-call(bf16[1,256,2048]{2,1,0:T(8,128)(2,1)} %q_hbm.1, bf16[1,256,2048]{2,1,0:T(8,128)(2,1)} %k_hbm.1, bf16[1,256,2048]{2,1,0:T(8,128)(2,1)} %v_hbm.1, ...), custom_call_target="tpu_custom_call" | custom-call | tf_op jit(solution)/shard_map/block/pallas_call | solution.py:602
  127.1 2.1 %store.1 = (bf16[1,256,2048]{2,1,0:T(8,128)(2,1)}, bf16[1,256,2048]{2,1,0:T(8,128)(2,1)}, bf16[1,256,2048]{2,1,0:T(8,128)(2,1)}, bf16[1,256,2048]{2,1,0:T(8,128)(2,1)}, f32[2,8,4096]{2,1,0:T(8,128)}) custom-call(bf16[256,2048]{1,0:T(8,128)(2,1)S(1)} %get-tuple-element.15.refs_0_, bf16[256,2048]{1,0:T(8,128)(2,1)S(1)} %get-tuple-element.16.refs_1_, ...), custom_call_target="tpu_custom_call" | custom-call | tf_op jit(solution)/shard_map/store/pallas_call | solution.py:614

commit v3 on v2

--- a/solution.py
+++ b/solution.py
@@ -21,13 +21,14 @@
 SEQ = ("seq_0", "seq_1", "seq_2")
 DP_SEQ = (DP,) + SEQ
 N_CHUNK = 4
-WIDTHS = (1536, 1280, 1280)
-STARTS = (0, 1536, 2816)
+WIDTHS = (1536, 1408, 1152)
+STARTS = (0, 1536, 2944)
 ORDERS = ((0, 1, 2), (1, 2, 0), (2, 0, 1))
 COL = 256
 W_ROWS = 256
 W_TILES = HD // W_ROWS
-VMEM_LIMIT = 62_000_000
+W_SLOTS = 3
+VMEM_LIMIT = 62_500_000
 
 
 def dot_nn(a, b):
@@ -75,7 +76,7 @@
     def copies(self, stage, c):
         out = []
         for r in range(1, 4):
-            s, v = self.ss.at[c, stage, r], self.rs.at[c, stage, r]
+            s, v = self.ss.at[stage], self.rs.at[c, stage]
             yt, xt, zt = (self.y + r) % 4, (self.x + r) % 4, (self.z + r) % 4
             if stage == 0:
                 out.append(send(self.S.at[yt, c], self.YR.at[c, self.y], s, v, {SEQ[2]: yt}))
@@ -90,20 +91,10 @@
         return out
 
     def landing(self, stage, c):
-        for r in range(1, 4):
-            s, v = self.ss.at[c, stage, r], self.rs.at[c, stage, r]
-            yf, xf, zf = (self.y + 4 - r) % 4, (self.x + 4 - r) % 4, (self.z + 4 - r) % 4
-            if stage == 0:
-                ref, dev = self.YR.at[c, yf], {SEQ[2]: yf}
-            elif stage == 1:
-                ref, dev = self.XR.at[c, xf], {SEQ[1]: xf}
-            elif stage == 2:
-                ref, dev = self.ZR.at[c, zf], {SEQ[0]: zf}
-            elif stage == 3:
-                ref, dev = self.XC.at[c, xf], {SEQ[1]: xf}
-            else:
-                ref, dev = self.R.at[yf, c], {SEQ[2]: yf}
-            send(ref, ref, s, v, dev).wait_recv()
+        ref = (
+            self.YR.at[c, 0:3], self.XR.at[c, 0:3], self.ZR.at[c, 0:3], self.XC.at[c, 0:3], self.R.at[0:3, c]
+        )[stage]
+        send(ref, ref, self.ss.at[stage], self.rs.at[c, stage], {SEQ[2]: (self.y + 1) % 4}).wait_recv()
 
     def go(self, stage, c):
         for copy in self.copies(stage, c):
@@ -151,9 +142,8 @@
             self.go(s, c)
 
     def drain(self, stage):
-        for c in range(N_CHUNK):
-            for copy in self.copies(stage, c):
-                copy.wait_send()
+        ref = (self.S.at[0:3], self.T.at[:, 0:3], self.T.at[:, 0:3], self.T.at[:, 0:3], self.S.at[0:3])[stage]
+        send(ref, ref, self.ss.at[stage], self.rs.at[0, stage], {SEQ[2]: (self.y + 1) % 4}).wait_send()
 
 
 class Color:
@@ -169,13 +159,15 @@
         for p in range(phase):
             idx[self.order[p]] = self.where[self.order[p]]
         idx[self.order[phase]] = t
-        if phase == 0:
-            nxt = self.order[1]
+        if phase < 2:
+            nxt = self.order[phase + 1]
             idx[nxt] = (self.where[nxt] + (2, 1, 3, 0)[u]) % 4
         return idx
 
-    def number(self, phase, kind, u):
-        return (kind * 4 + u) if phase == 0 else (24 + 6 * (phase - 1) + kind)
+    def sems(self, phase, kind, u):
+        leave = 4 * (kind // 2) + u if phase == 0 else 11 + phase
+        land = 8 * phase + 2 * u + (0 if kind < 2 else 1)
+        return self.ss.at[leave], self.rs.at[land]
 
     def copy(self, phase, kind, u=0):
         a = self.axis(phase)
@@ -184,22 +176,29 @@
         to = (m + 1) % 4 if up else (m + 3) % 4
         t = (m + 2) % 4 if kind < 2 else to
         half = (0, 1, 1, 0, 0, 1)[kind]
-        n = self.number(phase, kind, u)
         src = self.part.at[tuple(self.slot(phase, t, u)) + (half,)]
-        dst = self.recv[phase].at[kind, u] if phase == 0 else self.recv[phase].at[kind]
-        return send(src, dst, self.ss.at[n], self.rs.at[n], {SEQ[a]: to})
+        dst = self.recv[phase].at[kind, u] if phase < 2 else self.recv[phase].at[kind]
+        return send(src, dst, *self.sems(phase, kind, u), {SEQ[a]: to})
 
     def go(self, phase, kind, u=0):
         self.copy(phase, kind, u).start()
 
-    def left(self, phase, kind, u=0):
-        if (phase, kind, u) not in self.gone:
-            self.gone.add((phase, kind, u))
-            self.copy(phase, kind, u).wait_send()
+    def bulk(self, phase, kinds, u, ref):
+        a = self.axis(phase)
+        return send(ref, ref, *self.sems(phase, kinds.start, u), {SEQ[a]: (self.where[a] + 1) % 4})
+
+    def left(self, pair, u):
+        if (pair, u) not in self.gone:
+            self.gone.add((pair, u))
+            kinds = slice(2 * pair, 2 * pair + 2)
+            self.bulk(0, kinds, u, self.recv[0].at[kinds, u]).wait_send()
+
+    def landed(self, phase, kinds, u):
+        ref = self.recv[phase].at[kinds, u] if phase < 2 else self.recv[phase].at[kinds]
+        self.bulk(phase, kinds, u, ref).wait_recv()
 
     def got(self, phase, kind, u=0):
-        self.copy(phase, kind, u).wait_recv()
-        return self.recv[phase][kind, u] if phase == 0 else self.recv[phase][kind]
+        return self.recv[phase][kind, u] if phase < 2 else self.recv[phase][kind]
 
     def relay(self, phase, u=0):
         with jax.named_scope(f"relay{self.order[0]}_{phase}{u}"):
@@ -207,6 +206,7 @@
 
     def relay_in(self, phase, u=0):
         m = self.where[self.axis(phase)]
+        self.landed(phase, slice(0, 2), u)
         for kind, to, half in ((0, (m + 1) % 4, 0), (1, (m + 3) % 4, 1)):
             more = self.got(phase, kind, u)
             at = tuple(self.slot(phase, to, u)) + (half,)
@@ -219,6 +219,7 @@
 
     def finish_in(self, phase, u=0, to=None):
         m = self.where[self.axis(phase)]
+        self.landed(phase, slice(2, 6), u)
         for half, kinds in ((0, (3, 4)), (1, (2, 5))):
             more = self.got(phase, kinds[0], u) + self.got(phase, kinds[1], u)
             at = tuple(self.slot(phase, m, u)) + (half,)
@@ -228,12 +229,13 @@
                 out, start, width = to
                 out[half, :, start:start + width] = self.part[at] + more
 
-    def drain(self):
-        for kind in range(6):
-            for u in range(4):
-                self.left(0, kind, u)
-            for phase in (1, 2):
-                self.left(phase, kind)
+    def drain(self, phase):
+        if phase == 0:
+            for pair in range(3):
+                for u in range(4):
+                    self.left(pair, u)
+        else:
+            self.bulk(phase, slice(0, 6), 0, self.recv[phase]).wait_send()
 
 
 def kernel(
@@ -260,11 +262,11 @@
 
     def w_load(i):
         return pltpu.make_async_copy(
-            w_hbm.at[pl.ds(pl.multiple_of(i * W_ROWS, W_ROWS), W_ROWS)], w_v.at[i % 2], w_sem.at[i % 2]
+            w_hbm.at[pl.ds(pl.multiple_of(i * W_ROWS, W_ROWS), W_ROWS)], w_v.at[i % W_SLOTS], w_sem.at[i % W_SLOTS]
         )
 
-    w_load(0).start()
-    w_load(1).start()
+    for i in range(W_SLOTS):
+        w_load(i).start()
 
     barrier = pltpu.get_barrier_semaphore()
     pl.semaphore_signal(barrier, inc=1, device_id=other, device_id_type=MESH)
@@ -326,13 +328,13 @@
     def grad_tiles(lo, hi):
         def one(i, carry):
             w_load(i).wait()
-            block = dot_nt(og_v[:TOK], w_v[i % 2])
+            block = dot_nt(og_v[:TOK], w_v[i % W_SLOTS])
             at = pl.ds(pl.multiple_of(i * W_ROWS, W_ROWS), W_ROWS)
             grad_v[:, at] = block
 
-            @pl.when(i + 2 < W_TILES)
+            @pl.when(i + W_SLOTS < W_TILES)
             def _():
-                w_load(i + 2).start()
+                w_load(i + W_SLOTS).start()
             return carry
         lax.fori_loop(lo, hi, one, 0)
 
@@ -388,7 +390,7 @@
 
     def att_copies(c):
         return [
-            send(attS.at[2 * c + i], attR.at[2 * c + i], ats.at[2 * c + i], atr.at[2 * c + i], other)
+            send(attS.at[2 * c + i], attR.at[2 * c + i], ats.at[0], atr.at[c], other)
             for i in range(2)
         ]
 
@@ -401,9 +403,10 @@
 
     @scoped
     def att_take(c):
-        for i, copy in enumerate(att_copies(c)):
+        both = attR.at[2 * c:2 * c + 2]
+        send(both, both, ats.at[0], atr.at[c], other).wait_recv()
+        for i in range(2):
             hh = 4 * i + c
-            copy.wait_recv()
             attP[hh // 2, 2 * (hh % 2):2 * (hh % 2) + 2] = attR[2 * c + i].astype(BF16)
 
     forward = (
@@ -424,8 +427,6 @@
         forward_heads(c)
         scan2.step(0, c)
         att_give(c)
-        if c >= 2:
-            scan2.step(1, c - 2)
     for c in range(N_CHUNK):
         att_take(c)
     for i in range(3):
@@ -440,10 +441,10 @@
         idx[axis] = t
         idx = tuple(idx)
         both = jnp.concatenate([attT[(d,) + idx].reshape(TOK, TOK), attP[idx].reshape(TOK, TOK)], axis=1)
-        for n in range(WIDTHS[i] // COL):
-            at = STARTS[i] + n * COL
-            block = dot_nn(both, og_v[:, at:at + COL])
-            color.part[idx + (slice(None), slice(None), slice(n * COL, (n + 1) * COL))] = block.reshape(4, 4, 2, 8, COL)
+        for low in range(0, WIDTHS[i], COL):
+            high = min(low + COL, WIDTHS[i])
+            block = dot_nn(both, og_v[:, STARTS[i] + low:STARTS[i] + high])
+            color.part[idx + (slice(None), slice(None), slice(low, high))] = block.reshape(4, 4, 2, 8, high - low)
 
     @scoped
     def backward_heads(c):
@@ -472,46 +473,52 @@
 
     def paced(color, pair, u):
         n = 4 * pair + u - 2
-        for up in range(2):
-            color.left(0, 2 * (n // 4) + up, n % 4)
+        color.left(n // 4, n % 4)
         up_down(color, pair, u)
 
     for i in range(3):
         product(i, 2)
         up_down(colors[i], 0, 0)
         up_down(colors[i], 0, 1)
-    for offset in (1, 3, 0):
+    up_down(cz, 0, 2)
+    scan2.step(1, 0)
+    for i in range(3):
+        product(i, 1)
+    scan2.step(1, 1)
+    for offset in (3, 0):
         for i in range(3):
             product(i, offset)
+    paced(cx, 0, 2)
+    paced(cy, 0, 2)
     for item in ((1, 2), (1, 3), (2, 0), (2, 1)):
         scan2.step(*item)
+    for stage in range(1, 5):
+        scan1.drain(stage)
     for color in colors:
-        paced(color, 0, 2)
+        paced(color, 0, 3)
     for item in ((2, 2), (3, 0)):
         scan2.step(*item)
-    for color in colors:
-        paced(color, 0, 3)
+    paced(cx, 1, 0)
+    paced(cy, 1, 0)
     for item in ((2, 3), (3, 1)):
         scan2.step(*item)
     for u in range(4):
         up_down(cz, 1, u)
-    paced(cx, 1, 0)
-    paced(cy, 1, 0)
-    for item in ((4, 0), (3, 2)):
-        scan2.step(*item)
+    paced(cx, 1, 1)
+    scan2.step(4, 0)
+    scan2.step(3, 2)
+    paced(cx, 1, 2)
+    paced(cy, 1, 1)
     cz.relay(0, 0)
-    paced(cx, 1, 1)
-    paced(cy, 1, 1)
     cz.relay(0, 1)
+    scan2.step(4, 1)
+    scan2.step(3, 3)
+    up_down(cx, 1, 3)
     cz.relay(0, 2)
-    for item in ((4, 1), (3, 3)):
-        scan2.step(*item)
-    up_down(cx, 1, 2)
-    up_down(cx, 1, 3)
-    paced(cy, 1, 2)
     cz.relay(0, 3)
     for u in range(4):
         cx.relay(0, u)
+    paced(cy, 1, 2)
     scan2.step(4, 2)
     paced(cy, 1, 3)
     scan2.step(4, 3)
@@ -520,41 +527,50 @@
 
     def finish_first(color, u):
         color.finish(0, u)
-        if u == 0:
-            color.go(1, 0)
-            color.go(1, 1)
-        elif u == 1:
-            color.go(1, 2)
-        elif u == 2:
-            color.go(1, 3)
-
-    for u in range(4):
+        for v in range(4):
+            if u == 0:
+                color.go(1, 0, v)
+                color.go(1, 1, v)
+            elif u < 3:
+                color.go(1, 1 + u, v)
+
+    def finish_second(color, v):
+        color.finish(1, v)
+        if v == 0:
+            color.go(2, 0)
+            color.go(2, 1)
+        elif v < 3:
+            color.go(2, 1 + v)
+
+    for u in range(3):
         scan2.step(5, u)
         backward_heads(u)
-        finish_first(cz, u)
-        finish_first(cx, u)
-    for u in range(4):
-        finish_first(cy, u)
-    for color in colors:
-        color.relay(1)
-    for color in colors:
-        color.finish(1)
-        for kind in range(4):
-            color.go(2, kind)
-    for color in colors:
-        color.relay(2)
-    for i, color in enumerate(colors):
-        color.finish(2, to=(wg_v, STARTS[i], WIDTHS[i]))
-
-    for stage in range(1, 5):
-        scan1.drain(stage)
+    finish_first(cx, 0)
+    scan2.step(5, 3)
+    backward_heads(3)
+    for color, u in (
+        (cz, 0), (cx, 1), (cy, 0), (cz, 1), (cx, 2), (cy, 1), (cx, 3), (cz, 2), (cy, 2), (cz, 3), (cy, 3)
+    ):
+        finish_first(color, u)
     for stage in range(5):
         scan2.drain(stage)
+    send(attS, attS, ats.at[0], atr.at[0], other).wait_send()
     for color in colors:
-        color.drain()
-    for c in range(N_CHUNK):
-        for copy in att_copies(c):
-            copy.wait_send()
+        color.drain(0)
+    for v in range(4):
+        for color in (cx, cz, cy):
+            color.relay(1, v)
+    for v in range(4):
+        for color in (cx, cz, cy):
+            finish_second(color, v)
+    for color in colors:
+        color.drain(1)
+    for color in (cx, cz, cy):
+        color.relay(2)
+    for i in (1, 0, 2):
+        colors[i].finish(2, to=(wg_v, STARTS[i], WIDTHS[i]))
+    for color in colors:
+        color.drain(2)
 
 
 def store_kernel(*refs):
@@ -581,7 +597,7 @@
         ]
 
     scratch = [
-        vm((2 * TOK, D), BF16), vm((2, W_ROWS, D), BF16),
+        vm((2 * TOK, D), BF16), vm((W_SLOTS, W_ROWS, D), BF16),
         vm((TOK, HD), F32), vm((TOK, HD), F32), vm((TOK, HD), BF16),
         vm((2, 4, 4, 4, 16, TOK), BF16), vm((4, 4, 4, 16, TOK), BF16),
         vm((8, 2, 4, 16, TOK), F32), vm((8, 2, 4, 16, TOK), F32),
@@ -593,9 +609,9 @@
     scratch += [vm((6, 4, 8, w), F32) for w in WIDTHS]
     scratch += [vm((6, 8, w), F32) for w in WIDTHS]
     scratch += [
-        dma((4,)), dma((2,)),
-        dma((4, 5, 4)), dma((4, 5, 4)), dma((4, 5, 4)), dma((4, 5, 4)),
-        dma((3, 36)), dma((3, 36)), dma((3,)), dma((3,)), dma((8,)), dma((8,)),
+        dma((4,)), dma((W_SLOTS,)),
+        dma((5,)), dma((4, 5)), dma((5,)), dma((4, 5)),
+        dma((3, 14)), dma((3, 18)), dma((3,)), dma((3,)), dma((1,)), dma((4,)),
     ]
     any_space = pl.BlockSpec(memory_space=pl.ANY)
     in_vmem = pl.BlockSpec(memory_space=vm)

time: 130 us -> 121 us (0.931)
  Pallas kernels: 129 us -> 119 us
    pallas_call x1, Pallas kernels: 126 us -> 117 us  [body(): pl.pallas_call(kernel, out_shape=(vm((TOK, HD), BF16),) * 4 + (vm((2, 8,...]
where the time goes in v3:
time: 121 us; the launch traced here: 120 us
  Pallas kernels  119 us (98%)
    pallas_call x1, Pallas kernels, body(): pl.pallas_call(kernel, out_shape=(vm((TOK, HD), BF16),) * 4 + (vm((2, 8,...  117 us

profile of v3, /device:TPU:0, one launch (start us, length us, event | category | flops | bytes accessed | tf_op | source)
XLA Modules:
  0.0 120.0 jit_solution(4017925536054827417)
XLA Ops:
  0.6 117.1 %block.1 = (bf16[256,2048]{1,0:T(8,128)(2,1)S(1)}, bf16[256,2048]{1,0:T(8,128)(2,1)S(1)}, bf16[256,2048]{1,0:T(8,128)(2,1)S(1)}, bf16[256,2048]{1,0:T(8,128)(2,1)S(1)}, f32[2,8,4096]{2,1,0:T(8,128)S(1)}) custom-call(bf16[1,256,2048]{2,1,0:T(8,128)(2,1)} %q_hbm.1, bf16[1,256,2048]{2,1,0:T(8,128)(2,1)} %k_hbm.1, bf16[1,256,2048]{2,1,0:T(8,128)(2,1)} %v_hbm.1, ...), custom_call_target="tpu_custom_call" | custom-call | tf_op jit(solution)/shard_map/block/pallas_call | solution.py:618
  117.7 2.1 %store.1 = (bf16[1,256,2048]{2,1,0:T(8,128)(2,1)}, bf16[1,256,2048]{2,1,0:T(8,128)(2,1)}, bf16[1,256,2048]{2,1,0:T(8,128)(2,1)}, bf16[1,256,2048]{2,1,0:T(8,128)(2,1)}, f32[2,8,4096]{2,1,0:T(8,128)}) custom-call(bf16[256,2048]{1,0:T(8,128)(2,1)S(1)} %get-tuple-element.15.refs_0_, bf16[256,2048]{1,0:T(8,128)(2,1)S(1)} %get-tuple-element.16.refs_1_, ...), custom_call_target="tpu_custom_call" | custom-call | tf_op jit(solution)/shard_map/store/pallas_call | solution.py:630

commit v4 on v3

--- a/solution.py
+++ b/solution.py
@@ -58,7 +58,7 @@
 def scoped(f):
     @functools.wraps(f)
     def named(*args):
-        with jax.named_scope(f.__name__ + "_" + "".join(map(str, args))):
+        with jax.named_scope(f.__name__ + "_" + "".join(str(a) for a in args if isinstance(a, int))):
             return f(*args)
     return named
 
@@ -75,7 +75,7 @@
 
     def copies(self, stage, c):
         out = []
-        for r in range(1, 4):
+        for r in (2, 1, 3):
             s, v = self.ss.at[stage], self.rs.at[c, stage]
             yt, xt, zt = (self.y + r) % 4, (self.x + r) % 4, (self.z + r) % 4
             if stage == 0:
@@ -177,7 +177,7 @@
         t = (m + 2) % 4 if kind < 2 else to
         half = (0, 1, 1, 0, 0, 1)[kind]
         src = self.part.at[tuple(self.slot(phase, t, u)) + (half,)]
-        dst = self.recv[phase].at[kind, u] if phase < 2 else self.recv[phase].at[kind]
+        dst = self.recv[phase].at[kind, u]
         return send(src, dst, *self.sems(phase, kind, u), {SEQ[a]: to})
 
     def go(self, phase, kind, u=0):
@@ -194,11 +194,10 @@
             self.bulk(0, kinds, u, self.recv[0].at[kinds, u]).wait_send()
 
     def landed(self, phase, kinds, u):
-        ref = self.recv[phase].at[kinds, u] if phase < 2 else self.recv[phase].at[kinds]
-        self.bulk(phase, kinds, u, ref).wait_recv()
+        self.bulk(phase, kinds, u, self.recv[phase].at[kinds, u]).wait_recv()
 
     def got(self, phase, kind, u=0):
-        return self.recv[phase][kind, u] if phase < 2 else self.recv[phase][kind]
+        return self.recv[phase][kind, u]
 
     def relay(self, phase, u=0):
         with jax.named_scope(f"relay{self.order[0]}_{phase}{u}"):
@@ -213,21 +212,30 @@
             self.part[at] = self.part[at] + more
             self.go(phase, 4 + kind, u)
 
-    def finish(self, phase, u=0, to=None):
+    def finish(self, phase, u=0):
         with jax.named_scope(f"finish{self.order[0]}_{phase}{u}"):
-            self.finish_in(phase, u, to)
-
-    def finish_in(self, phase, u=0, to=None):
+            self.finish_in(phase, u)
+
+    def finish_in(self, phase, u=0):
         m = self.where[self.axis(phase)]
         self.landed(phase, slice(2, 6), u)
         for half, kinds in ((0, (3, 4)), (1, (2, 5))):
             more = self.got(phase, kinds[0], u) + self.got(phase, kinds[1], u)
             at = tuple(self.slot(phase, m, u)) + (half,)
-            if to is None:
-                self.part[at] = self.part[at] + more
-            else:
-                out, start, width = to
-                out[half, :, start:start + width] = self.part[at] + more
+            self.part[at] = self.part[at] + more
+
+    def direct(self, r):
+        a = self.axis(2)
+        to = (self.where[a] + r) % 4
+        src = self.part.at[tuple(self.slot(2, to, 0))]
+        return send(src, self.recv[2].at[r - 1], *self.sems(2, 0, 0), {SEQ[a]: to})
+
+    def last(self, out, start, width):
+        with jax.named_scope(f"last{self.order[0]}"):
+            self.bulk(2, slice(0, 6), 0, self.recv[2]).wait_recv()
+            own = self.part[tuple(self.slot(2, self.where[self.axis(2)], 0))]
+            total = (own + self.recv[2][0]) + (self.recv[2][1] + self.recv[2][2])
+            out[:, :, start:start + width] = total
 
     def drain(self, phase):
         if phase == 0:
@@ -257,16 +265,13 @@
         pltpu.make_async_copy(src.at[0], dst, in_sem.at[i])
         for i, (src, dst) in enumerate(((k_hbm, k_v), (v_hbm, v_v), (og_hbm, og_v.at[:TOK]), (q_hbm, q_v)))
     ]
-    for load in loads:
-        load.start()
+    loads[0].start()
+    loads[1].start()
 
     def w_load(i):
         return pltpu.make_async_copy(
             w_hbm.at[pl.ds(pl.multiple_of(i * W_ROWS, W_ROWS), W_ROWS)], w_v.at[i % W_SLOTS], w_sem.at[i % W_SLOTS]
         )
-
-    for i in range(W_SLOTS):
-        w_load(i).start()
 
     barrier = pltpu.get_barrier_semaphore()
     pl.semaphore_signal(barrier, inc=1, device_id=other, device_id_type=MESH)
@@ -302,6 +307,10 @@
     with jax.named_scope("load"):
         loads[0].wait()
         loads[1].wait()
+    loads[2].start()
+    for i in range(W_SLOTS):
+        w_load(i).start()
+    loads[3].start()
     states(0)
     with jax.named_scope("enter"):
         pl.semaphore_wait(barrier, 10)
@@ -422,21 +431,10 @@
         else:
             scan1.step(*item)
     scan1.drain(0)
-    for c in range(N_CHUNK):
-        scan1.step(5, c)
-        forward_heads(c)
-        scan2.step(0, c)
-        att_give(c)
-    for c in range(N_CHUNK):
-        att_take(c)
-    for i in range(3):
-        og_copy(i).wait_send()
-
-    @scoped
-    def product(i, offset):
+    @scoped
+    def product(i, t):
         color = colors[i]
         axis = ORDERS[i][0]
-        t = (where[axis] + offset) % 4
         idx = [slice(None)] * 3
         idx[axis] = t
         idx = tuple(idx)
@@ -476,53 +474,83 @@
         color.left(n // 4, n % 4)
         up_down(color, pair, u)
 
-    for i in range(3):
-        product(i, 2)
-        up_down(colors[i], 0, 0)
-        up_down(colors[i], 0, 1)
-    up_down(cz, 0, 2)
+    def early_and_late(kinds_even, kinds_odd, us):
+        for parity, kinds in ((0, kinds_even), (1, kinds_odd)):
+            @pl.when(z % 2 == parity)
+            def _(kinds=kinds):
+                for u in us:
+                    for kind in kinds:
+                        cz.go(0, kind, u)
+
+    for c in range(N_CHUNK):
+        scan1.step(5, c)
+        forward_heads(c)
+        scan2.step(0, c)
+        att_give(c)
+        if c == 2:
+            og_copy(0).wait_send()
+            att_take(0)
+            att_take(1)
+            product(0, 0)
+            product(0, 2)
+            early_and_late((0, 1), (2, 3), (0, 1, 2))
+    att_take(2)
+    att_take(3)
+    for i in (1, 2):
+        og_copy(i).wait_send()
+    product(1, (x + 2) % 4)
+    up_down(cx, 0, 0)
+    up_down(cx, 0, 1)
+    product(2, (y + 2) % 4)
+    for u in range(4):
+        up_down(cy, 0, u)
     scan2.step(1, 0)
-    for i in range(3):
-        product(i, 1)
+    product(1, (x + 1) % 4)
+    product(1, (x + 3) % 4)
+    product(2, (y + 1) % 4)
+    product(2, (y + 3) % 4)
+    up_down(cy, 1, 0)
+    up_down(cy, 1, 1)
     scan2.step(1, 1)
-    for offset in (3, 0):
-        for i in range(3):
-            product(i, offset)
+    product(0, 1)
+    product(0, 3)
+    product(1, x)
+    product(2, y)
+    scan2.step(1, 2)
+    scan2.step(1, 3)
     paced(cx, 0, 2)
-    paced(cy, 0, 2)
-    for item in ((1, 2), (1, 3), (2, 0), (2, 1)):
-        scan2.step(*item)
+    scan2.step(2, 0)
+    early_and_late((0, 1), (2, 3), (3,))
+    scan2.step(2, 1)
     for stage in range(1, 5):
         scan1.drain(stage)
-    for color in colors:
-        paced(color, 0, 3)
-    for item in ((2, 2), (3, 0)):
-        scan2.step(*item)
+    paced(cx, 0, 3)
+    scan2.step(2, 2)
+    early_and_late((2, 3), (0, 1), (0,))
+    scan2.step(3, 0)
     paced(cx, 1, 0)
-    paced(cy, 1, 0)
     for item in ((2, 3), (3, 1)):
         scan2.step(*item)
-    for u in range(4):
-        up_down(cz, 1, u)
+    early_and_late((2, 3), (0, 1), (1, 2, 3))
     paced(cx, 1, 1)
     scan2.step(4, 0)
     scan2.step(3, 2)
     paced(cx, 1, 2)
-    paced(cy, 1, 1)
+    paced(cy, 1, 2)
     cz.relay(0, 0)
-    cz.relay(0, 1)
     scan2.step(4, 1)
     scan2.step(3, 3)
     up_down(cx, 1, 3)
-    cz.relay(0, 2)
-    cz.relay(0, 3)
     for u in range(4):
         cx.relay(0, u)
-    paced(cy, 1, 2)
+    cz.relay(0, 1)
+    paced(cy, 1, 3)
     scan2.step(4, 2)
-    paced(cy, 1, 3)
+    cy.relay(0, 0)
+    cz.relay(0, 2)
     scan2.step(4, 3)
-    for u in range(4):
+    cz.relay(0, 3)
+    for u in range(1, 4):
         cy.relay(0, u)
 
     def finish_first(color, u):
@@ -536,20 +564,18 @@
 
     def finish_second(color, v):
         color.finish(1, v)
-        if v == 0:
-            color.go(2, 0)
-            color.go(2, 1)
-        elif v < 3:
-            color.go(2, 1 + v)
+        if v < 3:
+            color.direct((2, 1, 3)[v]).start()
 
     for u in range(3):
         scan2.step(5, u)
         backward_heads(u)
     finish_first(cx, 0)
+    finish_first(cz, 0)
     scan2.step(5, 3)
     backward_heads(3)
     for color, u in (
-        (cz, 0), (cx, 1), (cy, 0), (cz, 1), (cx, 2), (cy, 1), (cx, 3), (cz, 2), (cy, 2), (cz, 3), (cy, 3)
+        (cx, 1), (cy, 0), (cz, 1), (cx, 2), (cy, 1), (cx, 3), (cz, 2), (cy, 2), (cz, 3), (cy, 3)
     ):
         finish_first(color, u)
     for stage in range(5):
@@ -565,10 +591,8 @@
             finish_second(color, v)
     for color in colors:
         color.drain(1)
-    for color in (cx, cz, cy):
-        color.relay(2)
     for i in (1, 0, 2):
-        colors[i].finish(2, to=(wg_v, STARTS[i], WIDTHS[i]))
+        colors[i].last(wg_v, STARTS[i], WIDTHS[i])
     for color in colors:
         color.drain(2)
 
@@ -607,7 +631,7 @@
     ]
     scratch += [vm((6, 4, 4, 8, w), F32) for w in WIDTHS]
     scratch += [vm((6, 4, 8, w), F32) for w in WIDTHS]
-    scratch += [vm((6, 8, w), F32) for w in WIDTHS]
+    scratch += [vm((3, 2, 8, w), F32) for w in WIDTHS]
     scratch += [
         dma((4,)), dma((W_SLOTS,)),
         dma((5,)), dma((4, 5)), dma((5,)), dma((4, 5)),

time: 121 us -> 118 us (0.975)
  Pallas kernels: 119 us -> 116 us
    pallas_call x1, Pallas kernels: 117 us -> 114 us  [body(): pl.pallas_call(kernel, out_shape=(vm((TOK, HD), BF16),) * 4 + (vm((2, 8,...]
where the time goes in v4:
time: 118 us; the launch traced here: 117 us
  Pallas kernels  116 us (98%)
    pallas_call x1, Pallas kernels, body(): pl.pallas_call(kernel, out_shape=(vm((TOK, HD), BF16),) * 4 + (vm((2, 8,...  114 us

profile of v4, /device:TPU:0, one launch (start us, length us, event | category | flops | bytes accessed | tf_op | source)
XLA Modules:
  0.0 117.1 jit_solution(6300355730769566266)
XLA Ops:
  0.6 114.2 %block.1 = (bf16[256,2048]{1,0:T(8,128)(2,1)S(1)}, bf16[256,2048]{1,0:T(8,128)(2,1)S(1)}, bf16[256,2048]{1,0:T(8,128)(2,1)S(1)}, bf16[256,2048]{1,0:T(8,128)(2,1)S(1)}, f32[2,8,4096]{2,1,0:T(8,128)S(1)}) custom-call(bf16[1,256,2048]{2,1,0:T(8,128)(2,1)} %q_hbm.1, bf16[1,256,2048]{2,1,0:T(8,128)(2,1)} %k_hbm.1, bf16[1,256,2048]{2,1,0:T(8,128)(2,1)} %v_hbm.1, ...), custom_call_target="tpu_custom_call" | custom-call | tf_op jit(solution)/shard_map/block/pallas_call | solution.py:642
  114.8 2.1 %store.1 = (bf16[1,256,2048]{2,1,0:T(8,128)(2,1)}, bf16[1,256,2048]{2,1,0:T(8,128)(2,1)}, bf16[1,256,2048]{2,1,0:T(8,128)(2,1)}, bf16[1,256,2048]{2,1,0:T(8,128)(2,1)}, f32[2,8,4096]{2,1,0:T(8,128)}) custom-call(bf16[256,2048]{1,0:T(8,128)(2,1)S(1)} %get-tuple-element.15.refs_0_, bf16[256,2048]{1,0:T(8,128)(2,1)S(1)} %get-tuple-element.16.refs_1_, ...), custom_call_target="tpu_custom_call" | custom-call | tf_op jit(solution)/shard_map/store/pallas_call | solution.py:654

commit v5 on v4

--- a/solution.py
+++ b/solution.py
@@ -543,24 +543,23 @@
     up_down(cx, 1, 3)
     for u in range(4):
         cx.relay(0, u)
-    cz.relay(0, 1)
     paced(cy, 1, 3)
     scan2.step(4, 2)
     cy.relay(0, 0)
-    cz.relay(0, 2)
     scan2.step(4, 3)
-    cz.relay(0, 3)
     for u in range(1, 4):
         cy.relay(0, u)
+    cz.relay(0, 1)
+    cz.relay(0, 2)
 
     def finish_first(color, u):
         color.finish(0, u)
-        for v in range(4):
-            if u == 0:
+        if u == 0:
+            for v in range(4):
                 color.go(1, 0, v)
                 color.go(1, 1, v)
-            elif u < 3:
-                color.go(1, 1 + u, v)
+        elif u < 3:
+            color.go(1, 1 + u, 0)
 
     def finish_second(color, v):
         color.finish(1, v)
@@ -570,6 +569,8 @@
     for u in range(3):
         scan2.step(5, u)
         backward_heads(u)
+        if u == 0:
+            cz.relay(0, 3)
     finish_first(cx, 0)
     finish_first(cz, 0)
     scan2.step(5, 3)
@@ -586,6 +587,9 @@
     for v in range(4):
         for color in (cx, cz, cy):
             color.relay(1, v)
+            if v < 3:
+                color.go(1, 2, v + 1)
+                color.go(1, 3, v + 1)
     for v in range(4):
         for color in (cx, cz, cy):
             finish_second(color, v)

time: 118 us -> 117 us (level)
  no operation moved by 1% of the time
where the time goes in v5:
time: 117 us
  Pallas kernels  116 us (99%)
    pallas_call x1, Pallas kernels, body(): pl.pallas_call(kernel, out_shape=(vm((TOK, HD), BF16),) * 4 + (vm((2, 8,...  114 us

profile of v5, /device:TPU:0, one launch (start us, length us, event | category | flops | bytes accessed | tf_op | source)
XLA Modules:
  0.0 116.8 jit_solution(5386352550474895679)
XLA Ops:
  0.6 113.8 %block.1 = (bf16[256,2048]{1,0:T(8,128)(2,1)S(1)}, bf16[256,2048]{1,0:T(8,128)(2,1)S(1)}, bf16[256,2048]{1,0:T(8,128)(2,1)S(1)}, bf16[256,2048]{1,0:T(8,128)(2,1)S(1)}, f32[2,8,4096]{2,1,0:T(8,128)S(1)}) custom-call(bf16[1,256,2048]{2,1,0:T(8,128)(2,1)} %q_hbm.1, bf16[1,256,2048]{2,1,0:T(8,128)(2,1)} %k_hbm.1, bf16[1,256,2048]{2,1,0:T(8,128)(2,1)} %v_hbm.1, ...), custom_call_target="tpu_custom_call" | custom-call | tf_op jit(solution)/shard_map/block/pallas_call | solution.py:646
  114.5 2.1 %store.1 = (bf16[1,256,2048]{2,1,0:T(8,128)(2,1)}, bf16[1,256,2048]{2,1,0:T(8,128)(2,1)}, bf16[1,256,2048]{2,1,0:T(8,128)(2,1)}, bf16[1,256,2048]{2,1,0:T(8,128)(2,1)}, f32[2,8,4096]{2,1,0:T(8,128)}) custom-call(bf16[256,2048]{1,0:T(8,128)(2,1)S(1)} %get-tuple-element.15.refs_0_, bf16[256,2048]{1,0:T(8,128)(2,1)S(1)} %get-tuple-element.16.refs_1_, ...), custom_call_target="tpu_custom_call" | custom-call | tf_op jit(solution)/shard_map/store/pallas_call | solution.py:658

commit v6 on v5

--- a/solution.py
+++ b/solution.py
@@ -263,10 +263,13 @@
 
     loads = [
         pltpu.make_async_copy(src.at[0], dst, in_sem.at[i])
-        for i, (src, dst) in enumerate(((k_hbm, k_v), (v_hbm, v_v), (og_hbm, og_v.at[:TOK]), (q_hbm, q_v)))
+        for i, (src, dst) in enumerate(((og_hbm, og_v.at[:TOK]), (q_hbm, q_v)))
     ]
-    loads[0].start()
-    loads[1].start()
+    for first, size, sem in ((0, P_SIZE, 2), (P_SIZE, 3 * P_SIZE, 3)):
+        for j in range(4):
+            at = slice(4 * j * P_SIZE + first, 4 * j * P_SIZE + first + size)
+            for src, dst in ((k_hbm, k_v), (v_hbm, v_v)):
+                pltpu.make_async_copy(src.at[0, :, at], dst.at[:, at], in_sem.at[sem]).start()
 
     def w_load(i):
         return pltpu.make_async_copy(
@@ -305,21 +308,23 @@
         heads_of(some, c)
 
     with jax.named_scope("load"):
-        loads[0].wait()
-        loads[1].wait()
-    loads[2].start()
+        some = k_v.at[:, :HD // 2]
+        pltpu.make_async_copy(some, some, in_sem.at[2]).wait()
+    loads[0].start()
     for i in range(W_SLOTS):
         w_load(i).start()
-    loads[3].start()
+    loads[1].start()
     states(0)
     with jax.named_scope("enter"):
         pl.semaphore_wait(barrier, 10)
     scan1.step(0, 0)
+    rest = grad_v.at[:192]
+    pltpu.make_async_copy(rest, rest, in_sem.at[3]).wait()
     for c in range(1, N_CHUNK):
         states(c)
         scan1.step(0, c)
 
-    loads[2].wait()
+    loads[0].wait()
 
     def og_copy(i):
         return send(parts[i].at[0], parts[i].at[1], ogs.at[i], ogr.at[i], other)
@@ -424,7 +429,7 @@
         (3, 1), (2, 3), (4, 0), (inside_heads, 3), (3, 2), (4, 1), (3, 3), (og_take, 1), (4, 2), (og_take, 2),
         (4, 3),
     )
-    loads[3].wait()
+    loads[1].wait()
     for item in forward:
         if callable(item[0]):
             item[0](*item[1:])

time: 117 us -> 118 us (level)
  no operation moved by 1% of the time
where the time goes in v6:
time: 118 us; the launch traced here: 117 us
  Pallas kernels  116 us (98%)
    pallas_call x1, Pallas kernels, body(): pl.pallas_call(kernel, out_shape=(vm((TOK, HD), BF16),) * 4 + (vm((2, 8,...  114 us

profile of v6, /device:TPU:0, one launch (start us, length us, event | category | flops | bytes accessed | tf_op | source)
XLA Modules:
  0.0 116.8 jit_solution(4125483788015814227)
XLA Ops:
  0.6 113.9 %block.1 = (bf16[256,2048]{1,0:T(8,128)(2,1)S(1)}, bf16[256,2048]{1,0:T(8,128)(2,1)S(1)}, bf16[256,2048]{1,0:T(8,128)(2,1)S(1)}, bf16[256,2048]{1,0:T(8,128)(2,1)S(1)}, f32[2,8,4096]{2,1,0:T(8,128)S(1)}) custom-call(bf16[1,256,2048]{2,1,0:T(8,128)(2,1)} %q_hbm.1, bf16[1,256,2048]{2,1,0:T(8,128)(2,1)} %k_hbm.1, bf16[1,256,2048]{2,1,0:T(8,128)(2,1)} %v_hbm.1, ...), custom_call_target="tpu_custom_call" | custom-call | tf_op jit(solution)/shard_map/block/pallas_call | solution.py:651
  114.5 2.1 %store.1 = (bf16[1,256,2048]{2,1,0:T(8,128)(2,1)}, bf16[1,256,2048]{2,1,0:T(8,128)(2,1)}, bf16[1,256,2048]{2,1,0:T(8,128)(2,1)}, bf16[1,256,2048]{2,1,0:T(8,128)(2,1)}, f32[2,8,4096]{2,1,0:T(8,128)}) custom-call(bf16[256,2048]{1,0:T(8,128)(2,1)S(1)} %get-tuple-element.15.refs_0_, bf16[256,2048]{1,0:T(8,128)(2,1)S(1)} %get-tuple-element.16.refs_1_, ...), custom_call_target="tpu_custom_call" | custom-call | tf_op jit(solution)/shard_map/store/pallas_call | solution.py:663
